TPU v7x, 32 devices: a whole 2x2x4 slice. The times are simulated.
32 devices in a mesh: gx: 4 (over x, core), gy: 8 (over z, y).
Axes of the slice: x: 2, y: 2, z: 4, core: 2. Of those that a mesh axis runs over, the one named last changes fastest.
Arguments:
- normal_matrix: float32 [4096, 4096], P(('gx', 'gy')), may hold values from -1 to 4, as said below
- right_sides: float32 [4096, 32], P(('gx', 'gy')), may hold values from -6 to 6
- tile_order: int32 [32], replicated, may hold values from 0 to 31, as said below
- inner_order: int32 [32, 128], replicated, may hold values from 0 to 127, each once within a row
- block_lengths: int32 [16], replicated, may hold values from 1 to 3, as said below
Outputs:
- renumbered: float32 [4096, 4096], P(None, ('gx', 'gy'))
- solution: float32 [4096, 32], P(('gx', 'gy'))
Inputs may be any that keep to these rules, and one draw needn't show every extreme that they name: `normal_matrix`: symmetric positive definite. `tile_order`: a permutation. `inner_order`: each row a permutation. `block_lengths`: the lengths sum to 32, and the largest is 3.
All inputs are finite; a program needn't handle non-finite values.
Results may differ from a plain program's by a relative error of at most 0.0003.
Values sent between devices are 32-bit elements; how exact they have to be, the bound alone decides.
No kernel may reach another device: no remote copies, remote signals or barrier semaphores. Data moves between devices by JAX's collectives and lax.ppermute only.
A program may use at most 128 MiB of HBM per device.

v0:
```python
import jax
import jax.numpy as jnp
from jax import lax
from jax.sharding import PartitionSpec as P

MOSTT = 3


def from_behind(value, axis, steps):
    count = lax.axis_size(axis)
    leading, last = (max(0, -steps), min(count, count - steps))
    return lax.ppermute(value, axis, [(source, source + steps) for source in range(leading, last)])


def fetch_columns(window_piece, offset):
    return from_behind(window_piece, ("gx", "gy"), -offset)


def fetch_residual(residual, offset):
    return from_behind(residual, ("gx", "gy"), -offset)


def return_solution(solved_rows, offset):
    return from_behind(solved_rows, ("gx", "gy"), offset)


def body(normal_matrix, right_sides, tile_order, inner_order, block_lengths):
    tile_width = normal_matrix.shape[0]
    count_gx = lax.axis_size("gx")
    count_gy = lax.axis_size("gy")
    tile_count = count_gx * count_gy
    self_index = lax.axis_index(("gx", "gy"))
    new_to_old = (tile_order[:, None] * tile_width + inner_order).reshape(-1)
    row_slab = jnp.take(normal_matrix, new_to_old, axis=1)
    arrived = lax.all_to_all(row_slab, ("gx", "gy"), split_axis=1, concat_axis=0, tiled=True)
    column_slab = jnp.take(arrived, new_to_old, axis=0)
    sides_split = lax.all_to_all(right_sides, ("gx", "gy"), split_axis=1, concat_axis=0, tiled=True)
    sides_ordered = jnp.take(sides_split, new_to_old, axis=0)
    renumbered_sides = lax.all_to_all(
        sides_ordered, ("gx", "gy"), split_axis=0, concat_axis=1, tiled=True
    )
    starts = jnp.cumsum(block_lengths) - block_lengths
    block_index = jnp.sum((starts <= self_index).astype(jnp.int32)) - 1
    picked = jnp.arange(starts.shape[0]) == block_index
    first_tile = jnp.sum(jnp.where(picked, starts, 0))
    length = jnp.sum(jnp.where(picked, block_lengths, 0))
    position = self_index - first_tile
    block_span = length - position
    window_tile = jnp.minimum(first_tile, tile_count - MOSTT)
    lead_tiles = self_index - window_tile
    window_rows = MOSTT * tile_width
    window_piece = lax.dynamic_slice_in_dim(column_slab, window_tile * tile_width, window_rows, 0)
    window_pieces = [window_piece] + [
        fetch_columns(window_piece, offset) for offset in range(1, MOSTT)
    ]
    block_matrix = jnp.roll(
        jnp.concatenate(window_pieces, axis=1), -lead_tiles * tile_width, axis=0
    )
    tile_number = jnp.arange(window_rows) // tile_width
    inside = tile_number < block_span
    block_matrix = jnp.where(
        inside[:, None] & inside[None, :], block_matrix, jnp.eye(window_rows, dtype=jnp.float32)
    )
    factor = jnp.linalg.cholesky(block_matrix)

    def precondition(residual):
        gathered = [residual] + [fetch_residual(residual, offset) for offset in range(1, MOSTT)]
        stacked = jnp.where(inside[:, None], jnp.concatenate(gathered, axis=0), 0.0)
        solved = jax.scipy.linalg.cho_solve((factor, True), stacked)
        own_rows = solved[:tile_width]
        for offset in range(1, MOSTT):
            returned = return_solution(
                solved[offset * tile_width : (offset + 1) * tile_width], offset
            )
            own_rows = jnp.where(position == offset, returned, own_rows)
        return own_rows

    iterate = precondition(renumbered_sides)
    iterate = iterate + precondition(
        renumbered_sides
        - (
            jnp.zeros_like(iterate)
            + lax.dot_general(
                column_slab,
                lax.all_gather(iterate, ("gx", "gy"), axis=0, tiled=True),
                (((0,), (0,)), ((), ())),
                precision=lax.Precision.HIGHEST,
                preferred_element_type=jnp.float32,
            )
        )
    )
    return (column_slab, iterate)


def solution(mesh):
    placed = (P(("gx", "gy"), None), P(("gx", "gy"), None), P(), P(), P())
    return jax.shard_map(
        body,
        mesh=mesh,
        in_specs=placed,
        out_specs=(P(None, ("gx", "gy")), P(("gx", "gy"), None)),
        check_vma=False,
    )
```

profile of v0, /device:TPU:2, one launch (start us, length us, event | category | flops | bytes accessed | tf_op | source)
XLA Modules:
  0.0 353.6 jit_solution(17444266172508612999)
XLA Ops:
  0.6 6.1 %all-to-all-start.1 = ((f32[128,32,1]{0,2,1:T(1,128)}), f32[128,32,1]{0,2,1:T(1,128)S(1)}, u32[]{:S(2)}, u32[]{:S(2)}) async-start(f32[128,32,1]{0,2,1:T(1,128)} %bitcast.97), calls=%async_computation.1 | async-start | bytes 32768 | tf_op jit(solution)/shard_map/all_to_all | solution.py:37
  10.2 14.2 %gather_fusion = f32[4096,128]{1,0:T(8,128)} fusion(f32[128,4096]{0,1:T(8,128)S(1)} %copy.19, s32[4096]{0:T(1024)S(1)} %broadcast_clamp_fusion), kind=kCustom, calls=%fused_computation | custom fusion | bytes 4210688 | tf_op jit(solution)/shard_map/jit(_take)/gather | solution.py:34
  24.4 23.0 %gather_fusion.2 = f32[4096]{0:T(1024)S(1)} fusion(f32[4096]{0:T(1024)S(1)} %bitcast.87, s32[4096]{0:T(1024)S(1)} %broadcast_clamp_fusion), kind=kCustom, calls=%fused_computation.2 | custom fusion | bytes 49152 | tf_op jit(solution)/shard_map/jit(_take)/gather | solution.py:38
  48.0 5.8 %all-to-all-start.2 = ((f32[32,128,1]{1,2,0:T(1,128)}), f32[32,128,1]{1,2,0:T(1,128)S(1)}, u32[]{:S(2)}, u32[]{:S(2)}) async-start(f32[32,128,1]{1,2,0:T(1,128)} %bitcast.18), calls=%async_computation.2 | async-start | bytes 32768 | tf_op jit(solution)/shard_map/all_to_all | solution.py:39
  55.6 4.2 %all-to-all-done.2 = f32[32,128,1]{1,2,0:T(1,128)S(1)} async-done(((f32[32,128,1]{1,2,0:T(1,128)}), f32[32,128,1]{1,2,0:T(1,128)S(1)}, u32[]{:S(2)}, u32[]{:S(2)}) %all-to-all-start.2) | async-done | bytes 16416 | tf_op jit(solution)/shard_map/all_to_all | solution.py:39
  59.8 3.8 %all-to-all-start = ((f32[128,32,128]{0,2,1:T(8,128)}), f32[128,32,128]{0,2,1:T(8,128)S(1)}, u32[]{:S(2)}, u32[]{:S(2)}) async-start(f32[128,32,128]{0,2,1:T(8,128)} %broadcast_select_fusion.1), calls=%async_computation | async-start | bytes 4194304 | tf_op jit(solution)/shard_map/all_to_all | solution.py:35
  68.0 6.0 %collective-permute-start.2 = (f32[128,32]{0,1:T(8,128)S(1)}, f32[128,32]{0,1:T(8,128)S(1)}, u32[]{:S(2)}, u32[]{:S(2)}) collective-permute-start(f32[128,32]{0,1:T(8,128)S(1)} %bitcast.92), channel_id=1, source_target_pairs={{1,0},{2,1},{3,2},{4,3},{5,4},{6,5},{7,6},{8,7},{9,8},{10,9},{11,1... | collective-permute-start | bytes 49160 | tf_op jit(solution)/shard_map/ppermute | solution.py:12
  76.1 36.3 %all-to-all-done = f32[128,32,128]{0,2,1:T(8,128)S(1)} async-done(((f32[128,32,128]{0,2,1:T(8,128)}), f32[128,32,128]{0,2,1:T(8,128)S(1)}, u32[]{:S(2)}, u32[]{:S(2)}) %all-to-all-start) | async-done | bytes 2097184 | tf_op jit(solution)/shard_map/all_to_all | solution.py:35
  115.6 14.2 %gather_fusion.1 = f32[4096,128]{1,0:T(8,128)} fusion(f32[4096,128]{1,0:T(8,128)S(1)} %bitcast.88, s32[4096]{0:T(1024)S(1)} %broadcast_clamp_fusion), kind=kCustom, calls=%fused_computation.1 | custom fusion | bytes 4210688 | tf_op jit(solution)/shard_map/jit(_take)/gather | solution.py:36
  129.8 2.9 copy.21
  134.6 3.7 %collective-permute-start = (f32[384,128]{0,1:T(8,128)S(1)}, f32[384,128]{0,1:T(8,128)S(1)}, u32[]{:S(2)}, u32[]{:S(2)}) collective-permute-start(f32[384,128]{0,1:T(8,128)S(1)} %constant_dynamic-slice_fusion.1), channel_id=1, source_target_pairs={{1,0},{2,1},{3,2},{4,3},{5,4},{6,5},{7,6},{8,7},{9,8},{10,9},{11,1... | collective-permute-start | bytes 589832 | tf_op jit(solution)/shard_map/ppermute | solution.py:12
  140.7 3.1 collective-permute-done
  143.9 4.3 %collective-permute-done.1 = f32[384,128]{0,1:T(8,128)S(1)} collective-permute-done((f32[384,128]{0,1:T(8,128)S(1)}, f32[384,128]{0,1:T(8,128)S(1)}, u32[]{:S(2)}, u32[]{:S(2)}) %collective-permute-start.1) | collective-permute-done | bytes 196640 | tf_op jit(solution)/shard_map/ppermute | solution.py:12
  150.0 11.7 %cholesky.77 = f32[128,128]{1,0:T(8,128)S(1)} custom-call(f32[128,128]{1,0:T(8,128)S(1)} %cholesky.192), custom_call_target="Cholesky" | custom-call | tf_op jit(solution)/shard_map/jit(cholesky)/cholesky | solution.py:64
  161.8 9.8 %custom-call.24 = f32[1,128,128]{1,2,0:T(8,128)S(1)} custom-call(f32[1,128,128]{2,1,0:T(8,128)S(1)} %get-tuple-element.47), custom_call_target="InvertDiagBlocksLowerTriangular" | custom-call | tf_op jit(solution)/shard_map/jit(cholesky)/cholesky | solution.py:64
  174.0 11.7 %cholesky.162 = f32[128,128]{1,0:T(8,128)S(1)} custom-call(f32[128,128]{1,0:T(8,128)S(1)} %cholesky.196), custom_call_target="Cholesky" | custom-call | tf_op jit(solution)/shard_map/jit(cholesky)/cholesky | solution.py:64
  187.1 10.0 %custom-call.25 = f32[1,128,128]{1,2,0:T(8,128)S(1)} custom-call(f32[1,128,128]{2,1,0:T(8,128)S(1)} %get-tuple-element.44), custom_call_target="InvertDiagBlocksLowerTriangular" | custom-call | tf_op jit(solution)/shard_map/jit(cholesky)/cholesky | solution.py:64
  198.4 11.7 %cholesky.181 = f32[128,128]{1,0:T(8,128)S(1)} custom-call(f32[128,128]{1,0:T(8,128)S(1)} %convolution_subtract_fusion.1), custom_call_target="Cholesky" | custom-call | tf_op jit(solution)/shard_map/jit(cholesky)/cholesky | solution.py:64
  212.8 6.4 %while.4 = (s32[]{:T(128)}, f32[384,384]{1,0:T(8,128)S(1)}, s32[3,2]{0,1:T(2,128)S(1)}, f32[3,128,128]{2,1,0:T(8,128)S(1)}, s32[]{:T(128)}) while((s32[]{:T(128)}, f32[384,384]{1,0:T(8,128)S(1)}, s32[3,2]{0,1:T(2,128)S(1)}, f32[3,128,128]{2,1,0:T(8,128)S(1)}, s32[]{:T(128)}) %tuple.40), condition=%wide.while_cond, body=%wide.while_body.sunk | while | flops 2 | bytes 131181 | solution.py:69
  219.1 29.5 %custom-call.27 = f32[3,128,128]{1,2,0:T(8,128)S(1)} custom-call(f32[3,128,128]{2,1,0:T(8,128)S(1)} %get-tuple-element.17), custom_call_target="InvertDiagBlocksLowerTriangular" | custom-call | tf_op jit(solution)/shard_map/jit(_cho_solve)/triangular_solve | solution.py:69
  254.3 6.5 %collective-permute-done.5 = f32[128,32]{0,1:T(8,128)S(1)} collective-permute-done((f32[128,32]{0,1:T(8,128)S(1)}, f32[128,32]{0,1:T(8,128)S(1)}, u32[]{:S(2)}, u32[]{:S(2)}) %collective-permute-start.5) | collective-permute-done | bytes 16416 | tf_op jit(solution)/shard_map/ppermute | solution.py:12
  261.0 66.2 %all_gather.3 = f32[4096,32]{0,1:T(8,128)S(1)} all-gather(f32[128,32]{0,1:T(8,128)S(1)} %fusion.2), channel_id=1, replica_groups=mesh['gx'=4,'gy'=8] {'gx','gy'}, dimensions={0}, use_global_device_ids=true | all-gather | bytes 540672 | tf_op jit(solution)/shard_map/all_gather | solution.py:85
  339.9 3.9 %collective-permute-start.8 = (f32[128,32]{0,1:T(8,128)S(1)}, f32[128,32]{0,1:T(8,128)S(1)}, u32[]{:S(2)}, u32[]{:S(2)}) collective-permute-start(f32[128,32]{0,1:T(8,128)S(1)} %fusion.29), channel_id=1, source_target_pairs={{0,2},{1,3},{2,4},{3,5},{4,6},{5,7},{6,8},{7,9},{8,10},{9,11},{10,... | collective-permute-start | bytes 49160 | tf_op jit(solution)/shard_map/ppermute | solution.py:12
  346.2 6.5 %collective-permute-done.9 = f32[128,32]{0,1:T(8,128)S(1)} collective-permute-done((f32[128,32]{0,1:T(8,128)S(1)}, f32[128,32]{0,1:T(8,128)S(1)}, u32[]{:S(2)}, u32[]{:S(2)}) %collective-permute-start.9) | collective-permute-done | bytes 16416 | tf_op jit(solution)/shard_map/ppermute | solution.py:12
  (91 shorter events, 52.5 us)
Async XLA Ops:
  0.6 23.8 %all-to-all-start.1 = ((f32[128,32,1]{0,2,1:T(1,128)}), f32[128,32,1]{0,2,1:T(1,128)S(1)}, u32[]{:S(2)}, u32[]{:S(2)}) async-start(f32[128,32,1]{0,2,1:T(1,128)} %bitcast.97), calls=%async_computation.1 | async-start | bytes 32768 | tf_op jit(solution)/shard_map/all_to_all | solution.py:37
  24.4 29.5 %copy-start.1 = (f32[4096,128]{1,0:T(8,128)S(1)}, f32[4096,128]{1,0:T(8,128)}, u32[]{:S(2)}) copy-start(f32[4096,128]{1,0:T(8,128)} %gather_fusion) | copy-start | bytes 6291460
  48.0 11.7 %all-to-all-start.2 = ((f32[32,128,1]{1,2,0:T(1,128)}), f32[32,128,1]{1,2,0:T(1,128)S(1)}, u32[]{:S(2)}, u32[]{:S(2)}) async-start(f32[32,128,1]{1,2,0:T(1,128)} %bitcast.18), calls=%async_computation.2 | async-start | bytes 32768 | tf_op jit(solution)/shard_map/all_to_all | solution.py:39
  55.6 8.0 %copy-start.3 = (s32[16]{0:T(128)S(1)}, s32[16]{0:T(128)}, u32[]{:S(2)}) copy-start(s32[16]{0:T(128)} %param.11) | copy-start | bytes 196
  59.8 52.6 %all-to-all-start = ((f32[128,32,128]{0,2,1:T(8,128)}), f32[128,32,128]{0,2,1:T(8,128)S(1)}, u32[]{:S(2)}, u32[]{:S(2)}) async-start(f32[128,32,128]{0,2,1:T(8,128)} %broadcast_select_fusion.1), calls=%async_computation | async-start | bytes 4194304 | tf_op jit(solution)/shard_map/all_to_all | solution.py:35
  68.0 72.7 %collective-permute-start.2 = (f32[128,32]{0,1:T(8,128)S(1)}, f32[128,32]{0,1:T(8,128)S(1)}, u32[]{:S(2)}, u32[]{:S(2)}) collective-permute-start(f32[128,32]{0,1:T(8,128)S(1)} %bitcast.92), channel_id=1, source_target_pairs={{1,0},{2,1},{3,2},{4,3},{5,4},{6,5},{7,6},{8,7},{9,8},{10,9},{11,1... | collective-permute-start | bytes 49160 | tf_op jit(solution)/shard_map/ppermute | solution.py:12
  74.0 66.7 %collective-permute-start.3 = (f32[128,32]{0,1:T(8,128)S(1)}, f32[128,32]{0,1:T(8,128)S(1)}, u32[]{:S(2)}, u32[]{:S(2)}) collective-permute-start(f32[128,32]{0,1:T(8,128)S(1)} %bitcast.93), channel_id=1, source_target_pairs={{2,0},{3,1},{4,2},{5,3},{6,4},{7,5},{8,6},{9,7},{10,8},{11,9},{12,... | collective-permute-start | bytes 49160 | tf_op jit(solution)/shard_map/ppermute | solution.py:12
  112.4 1.3 copy-start
  134.6 9.3 %collective-permute-start = (f32[384,128]{0,1:T(8,128)S(1)}, f32[384,128]{0,1:T(8,128)S(1)}, u32[]{:S(2)}, u32[]{:S(2)}) collective-permute-start(f32[384,128]{0,1:T(8,128)S(1)} %constant_dynamic-slice_fusion.1), channel_id=1, source_target_pairs={{1,0},{2,1},{3,2},{4,3},{5,4},{6,5},{7,6},{8,7},{9,8},{10,9},{11,1... | collective-permute-start | bytes 589832 | tf_op jit(solution)/shard_map/ppermute | solution.py:12
  138.3 9.9 %collective-permute-start.1 = (f32[384,128]{0,1:T(8,128)S(1)}, f32[384,128]{0,1:T(8,128)S(1)}, u32[]{:S(2)}, u32[]{:S(2)}) collective-permute-start(f32[384,128]{0,1:T(8,128)S(1)} %constant_dynamic-slice_fusion.1), channel_id=1, source_target_pairs={{2,0},{3,1},{4,2},{5,3},{6,4},{7,5},{8,6},{9,7},{10,8},{11,9},{12,... | collective-permute-start | bytes 589832 | tf_op jit(solution)/shard_map/ppermute | solution.py:12
  149.2 0.8 copy-start.2
  250.0 10.8 %collective-permute-start.4 = (f32[128,32]{0,1:T(8,128)S(1)}, f32[128,32]{0,1:T(8,128)S(1)}, u32[]{:S(2)}, u32[]{:S(2)}) collective-permute-start(f32[128,32]{0,1:T(8,128)S(1)} %fusion.31), channel_id=1, source_target_pairs={{0,2},{1,3},{2,4},{3,5},{4,6},{5,7},{6,8},{7,9},{8,10},{9,11},{10,... | collective-permute-start | bytes 49160 | tf_op jit(solution)/shard_map/ppermute | solution.py:12
  252.2 8.7 %collective-permute-start.5 = (f32[128,32]{0,1:T(8,128)S(1)}, f32[128,32]{0,1:T(8,128)S(1)}, u32[]{:S(2)}, u32[]{:S(2)}) collective-permute-start(f32[128,32]{0,1:T(8,128)S(1)} %fusion.37), channel_id=1, source_target_pairs={{0,1},{1,2},{2,3},{3,4},{4,5},{5,6},{6,7},{7,8},{8,9},{9,10},{10,1... | collective-permute-start | bytes 49160 | tf_op jit(solution)/shard_map/ppermute | solution.py:12
  329.3 6.5 %collective-permute-start.6 = (f32[128,32]{0,1:T(8,128)S(1)}, f32[128,32]{0,1:T(8,128)S(1)}, u32[]{:S(2)}, u32[]{:S(2)}) collective-permute-start(f32[128,32]{0,1:T(8,128)S(1)} %convolution_subtract_fusion.6), channel_id=1, source_target_pairs={{1,0},{2,1},{3,2},{4,3},{5,4},{6,5},{7,6},{8,7},{9,8},{10,9},{11,1... | collective-permute-start | bytes 49160 | tf_op jit(solution)/shard_map/ppermute | solution.py:12
  332.0 6.5 %collective-permute-start.7 = (f32[128,32]{0,1:T(8,128)S(1)}, f32[128,32]{0,1:T(8,128)S(1)}, u32[]{:S(2)}, u32[]{:S(2)}) collective-permute-start(f32[128,32]{0,1:T(8,128)S(1)} %convolution_subtract_fusion.6), channel_id=1, source_target_pairs={{2,0},{3,1},{4,2},{5,3},{6,4},{7,5},{8,6},{9,7},{10,8},{11,9},{12,... | collective-permute-start | bytes 49160 | tf_op jit(solution)/shard_map/ppermute | solution.py:12
  339.9 12.8 %collective-permute-start.8 = (f32[128,32]{0,1:T(8,128)S(1)}, f32[128,32]{0,1:T(8,128)S(1)}, u32[]{:S(2)}, u32[]{:S(2)}) collective-permute-start(f32[128,32]{0,1:T(8,128)S(1)} %fusion.29), channel_id=1, source_target_pairs={{0,2},{1,3},{2,4},{3,5},{4,6},{5,7},{6,8},{7,9},{8,10},{9,11},{10,... | collective-permute-start | bytes 49160 | tf_op jit(solution)/shard_map/ppermute | solution.py:12
  344.1 8.7 %collective-permute-start.9 = (f32[128,32]{0,1:T(8,128)S(1)}, f32[128,32]{0,1:T(8,128)S(1)}, u32[]{:S(2)}, u32[]{:S(2)}) collective-permute-start(f32[128,32]{0,1:T(8,128)S(1)} %fusion.35), channel_id=1, source_target_pairs={{0,1},{1,2},{2,3},{3,4},{4,5},{5,6},{6,7},{7,8},{8,9},{9,10},{10,1... | collective-permute-start | bytes 49160 | tf_op jit(solution)/shard_map/ppermute | solution.py:12
where the time goes:
time: 354 us
  other arithmetic  94.5 us (27%)
  local copies, waits for them, and re-layouts  68.8 us (19%)
  blocking collectives  66.2 us (19%)
  waiting for transfers between devices  63.8 us (18%)
  starting transfers between devices  44.3 us (13%)
  matrix products  10.2 us (3%)
  between operations  5.73 us (2%)
    all_gather x1, blocking collectives, body(): lax.all_gather(iterate, ('gx', 'gy'), axis=0, tiled=True)  66.2 us
    another operation x11, other arithmetic, body(): factor = jnp.linalg.cholesky(block_matrix)  57 us
    all_to_all x1, waiting for transfers between devices, body(): lax.all_to_all(row_slab, ('gx', 'gy'), split_axis=1, concat_axis=0, tiled...  36.3 us
    another operation x4, other arithmetic, precondition(): solved = jax.scipy.linalg.cho_solve((factor, True), stacked)  29.5 us
    ppermute x10, starting transfers between devices, from_behind(): lax.ppermute(value, axis, [(source, source + steps) for source in range(l...  28.6 us
    ppermute x10, waiting for transfers between devices, from_behind(): lax.ppermute(value, axis, [(source, source + steps) for source in range(l...  23.3 us
    gather x1, local copies, waits for them, and re-layouts, body(): sides_ordered = jnp.take(sides_split, new_to_old, axis=0)  23 us
    gather x2, local copies, waits for them, and re-layouts, body(): column_slab = jnp.take(arrived, new_to_old, axis=0)  17.1 us
  transfers between devices with their start and end apart: 13, of which 7 were waited for; matrix products, arithmetic and copies ran while one was open for 13% of the time, Pallas kernels for 0%

commit v1 on v0

v1 whole, which is shorter than its diff:
```python
import jax
import jax.numpy as jnp
from jax import lax
from jax.experimental import pallas as pl
from jax.experimental.pallas import tpu as pltpu
from jax.sharding import PartitionSpec as P

MOSTT = 3
AXES = ("gx", "gy")
SUB = 8
HIGHEST = lax.Precision.HIGHEST


def dot(a, b, contract=((1,), (0,))):
    return lax.dot_general(
        a, b, (contract, ((), ())), precision=HIGHEST, preferred_element_type=jnp.float32
    )


def dot_t(a, b):
    return dot(a, b, ((1,), (1,)))


def one_pass(a, b):
    return lax.dot_general(a, b, (((1,), (0,)), ((), ())), preferred_element_type=jnp.float32)


def place_of_tile(order_ref, tiles, old_tile):
    def step(t, found):
        return jnp.where(order_ref[t] == old_tile, t, found)

    return lax.fori_loop(0, tiles, step, jnp.int32(0))


def block_of(lengths_ref, place):
    def step(e, carry):
        start, first, length = carry
        here = (start <= place) & (place < start + lengths_ref[e])
        first = jnp.where(here, start, first)
        length = jnp.where(here, lengths_ref[e], length)
        return start + lengths_ref[e], first, length

    zero = jnp.int32(0)
    _, first, length = lax.fori_loop(0, lengths_ref.shape[0], step, (zero, zero, zero + 1))
    return first, length


def pack_body(self_ref, order_ref, lengths_ref, inner_ref, slab_ref, sides_ref, send_ref, small_ref, rows_ref):
    tile = slab_ref.shape[0]
    tiles = order_ref.shape[0]
    rhs = sides_ref.shape[1]
    place = place_of_tile(order_ref, tiles, self_ref[0])
    first, length = block_of(lengths_ref, place)
    position = place - first
    own_inner = inner_ref[pl.ds(place, 1), :]
    hot = jnp.where(
        lax.broadcasted_iota(jnp.int32, (tile, tile), 0) == own_inner, 1.0, 0.0
    )
    row_hot = hot.T.astype(jnp.bfloat16)
    width = slab_ref.shape[1]
    step = min(width, 8 * tile)

    def order_rows(c, _):
        at = pl.ds(pl.multiple_of(c * step, step), step)
        x = slab_ref[:, at]
        high = x.astype(jnp.bfloat16)
        rest = x - high.astype(jnp.float32)
        middle = rest.astype(jnp.bfloat16)
        low = (rest - middle.astype(jnp.float32)).astype(jnp.bfloat16)
        rows_ref[:, at] = (one_pass(row_hot, low) + one_pass(row_hot, middle)) + one_pass(row_hot, high)
        return 0

    lax.fori_loop(0, width // step, order_rows, 0)

    def order_columns(t, _):
        at = pl.ds(pl.multiple_of(order_ref[t] * tile, tile), tile)
        chosen = jnp.broadcast_to(inner_ref[pl.ds(t, 1), :], (SUB, tile))
        for g in range(tile // SUB):
            x = rows_ref[g * SUB : (g + 1) * SUB, at]
            send_ref[t, g * SUB : (g + 1) * SUB, :] = jnp.take_along_axis(x, chosen, axis=1)
        return 0

    lax.fori_loop(0, tiles, order_columns, 0)

    after = jnp.where(position == MOSTT - 1, 0, position + 1)
    beside = jnp.minimum(first + after, tiles - 1)
    turned = sides_ref[...].T
    sides_turned = jnp.take_along_axis(turned, jnp.broadcast_to(own_inner, (rhs, tile)), axis=1)
    pieces = 2 * tile // SUB
    per_piece = rhs // pieces
    for k in range(pieces):
        if k < pieces // 2:
            chunk = send_ref[place, k * SUB : (k + 1) * SUB, :]
        else:
            at = (k - pieces // 2) * SUB
            chunk = send_ref[beside, at : at + SUB, :]
        small_ref[k, 0:SUB, :] = chunk
        small_ref[k, SUB : 2 * SUB, :] = jnp.zeros((SUB, tile), jnp.float32)
        small_ref[k, SUB : SUB + per_piece, :] = sides_turned[k * per_piece : (k + 1) * per_piece, :]
    for k in range(pieces, tiles):
        small_ref[k] = jnp.zeros(small_ref.shape[1:], jnp.float32)


def route_body(order_ref, lengths_ref, got_ref, send_ref, first_ref, *, per_piece):
    tiles = order_ref.shape[0]

    def block(e, start):
        for j in range(MOSTT):
            @pl.when(j < lengths_ref[e])
            def _():
                first_ref[start + j] = start
        return start + lengths_ref[e]

    lax.fori_loop(0, lengths_ref.shape[0], block, jnp.int32(0))
    spare = send_ref.shape[1] - MOSTT * SUB

    def fill(d, _):
        send_ref[d, MOSTT * SUB :, :] = jnp.zeros((spare, send_ref.shape[2]), jnp.float32)
        for m in range(MOSTT):
            source = order_ref[jnp.minimum(first_ref[d] + m, tiles - 1)]
            send_ref[d, m * SUB : (m + 1) * SUB, :] = got_ref[source, 0:SUB, :]
            at = MOSTT * SUB + m * per_piece
            send_ref[d, at : at + per_piece, :] = got_ref[source, SUB : SUB + per_piece, :]
        return 0

    lax.fori_loop(0, tiles, fill, 0)


def sweep(s):
    for k in range(SUB):
        inverse = pltpu.reciprocal(s[k][k], approx=False)
        column = [s[max(i, k)][min(i, k)] for i in range(SUB)]
        scaled = [column[i] * inverse for i in range(SUB)]
        for i in range(SUB):
            for j in range(i + 1):
                if i != k and j != k:
                    s[i][j] = s[i][j] - scaled[i] * column[j]
        for i in range(SUB):
            if i != k:
                s[max(i, k)][min(i, k)] = scaled[i]
        s[k][k] = -inverse
    return s


def invert_in_place(m_ref):
    size = m_ref.shape[0]
    lane = lax.broadcasted_iota(jnp.int32, (SUB, size), 1)
    sub = lax.broadcasted_iota(jnp.int32, (SUB, size), 0)

    def panel(p, _):
        row = pl.multiple_of(p * SUB, SUB)
        rows = m_ref[pl.ds(row, SUB), :]
        inside = (lane >= row) & (lane < row + SUB)
        at = [jnp.full((SUB, size), row + j, jnp.int32) for j in range(SUB)]
        columns = [jnp.take_along_axis(rows, at[j], axis=1) for j in range(SUB)]
        s = [
            [jnp.broadcast_to(columns[j][i : i + 1, :], (SUB, size)) for j in range(i + 1)]
            for i in range(SUB)
        ]
        s = sweep(s)
        spread = [
            jnp.where(
                inside,
                jnp.where(lane == row + j, 1.0, 0.0),
                jnp.broadcast_to(rows[j : j + 1, :], (SUB, size)),
            )
            for j in range(SUB)
        ]
        update = []
        for i in range(SUB):
            total = s[i][0] * spread[0]
            for j in range(1, SUB):
                total = total + s[max(i, j)][min(i, j)] * spread[j]
            update.append(total)
        new = -update[0]
        for i in range(1, SUB):
            new = jnp.where(sub == i, -update[i], new)
        for g in range(size // SUB):
            here = m_ref[g * SUB : (g + 1) * SUB, :]
            total = jnp.where(inside, 0.0, here)
            for j in range(SUB):
                total = total + jnp.take_along_axis(here, at[j], axis=1) * update[j]
            m_ref[g * SUB : (g + 1) * SUB, :] = total
        m_ref[pl.ds(row, SUB), :] = new
        return 0

    lax.fori_loop(0, size // SUB, panel, 0)


def apply_inverse(f_ref, b):
    y1 = b[1] - dot(b[0], f_ref[3])
    y2 = b[2] - dot(b[0], f_ref[4]) - dot(y1, f_ref[5])
    z2 = dot(y2, f_ref[2])
    z1 = dot(y1, f_ref[1]) - dot_t(z2, f_ref[5])
    z0 = dot(b[0], f_ref[0]) - dot_t(z1, f_ref[3]) - dot_t(z2, f_ref[4])
    return z0, z1, z2


def pick(position, values):
    chosen = values[0]
    for m in range(1, len(values)):
        chosen = jnp.where(position == m, values[m], chosen)
    return chosen


def factor_body(self_ref, lengths_ref, got_ref, f_ref, b_ref, z_ref, zs_ref, o_ref, bs_ref, *, per_piece):
    tile = got_ref.shape[2]
    pieces = 2 * tile // SUB
    place = self_ref[0]
    first, length = block_of(lengths_ref, place)
    position = place - first
    eye = jnp.where(
        lax.broadcasted_iota(jnp.int32, (SUB, tile), 0)
        == lax.broadcasted_iota(jnp.int32, (SUB, tile), 1),
        1.0,
        0.0,
    )
    lane = lax.broadcasted_iota(jnp.int32, (SUB, tile), 1)
    sub = lax.broadcasted_iota(jnp.int32, (SUB, tile), 0)
    for m in range(MOSTT):
        pair_inside = m + 1 < length if m < MOSTT - 1 else m < length
        for k in range(pieces // 2):
            diagonal = jnp.where(lane == sub + k * SUB, 1.0, 0.0)
            at = slice(k * SUB, (k + 1) * SUB)
            f_ref[m, at, :] = jnp.where(m < length, got_ref[k, m * SUB : (m + 1) * SUB, :], diagonal)
            beside = got_ref[k + pieces // 2, m * SUB : (m + 1) * SUB, :]
            o_ref[m, at, :] = jnp.where(pair_inside, beside, 0.0)
        for k in range(pieces):
            start = MOSTT * SUB + m * per_piece
            part = got_ref[k, start : start + per_piece, :]
            bs_ref[m, k * per_piece : (k + 1) * per_piece, :] = jnp.where(m < length, part, 0.0)
    a01 = o_ref[0]
    a12 = o_ref[1]
    a20 = o_ref[2]
    a10 = a01.T
    invert_in_place(f_ref.at[0])
    w01 = dot(f_ref[0], a01)
    w02 = dot_t(f_ref[0], a20)
    f_ref[3] = w01
    f_ref[4] = w02
    f_ref[1] = f_ref[1] - dot(a10, w01)
    s12 = a12 - dot(a10, w02)
    invert_in_place(f_ref.at[1])
    w12 = dot(f_ref[1], s12)
    f_ref[5] = w12
    f_ref[2] = f_ref[2] - dot(a20, w02) - dot(s12.T, w12)
    invert_in_place(f_ref.at[2])
    b = [bs_ref[m] for m in range(MOSTT)]
    z = pick(position, apply_inverse(f_ref, b))
    b_ref[...] = pick(position, b)
    z_ref[...] = z
    for d in range(zs_ref.shape[0]):
        zs_ref[d] = z


def arrange_body(order_ref, got_ref, slab_ref):
    tiles = order_ref.shape[0]
    tile = got_ref.shape[1]

    def move(t, _):
        slab_ref[pl.ds(pl.multiple_of(t * tile, tile), tile), :] = got_ref[order_ref[t]]
        return 0

    lax.fori_loop(0, tiles, move, 0)


def residual_body(slab_ref, iterate_ref, b_ref, r_ref):
    tiles, rhs, tile = iterate_ref.shape
    group = 8
    total = b_ref[...]
    for c in range(tiles // group):
        x = jnp.concatenate([iterate_ref[c * group + t] for t in range(group)], axis=1)
        total = total - dot(x, slab_ref[c * group * tile : (c + 1) * group * tile, :])
    r_ref[...] = total


def finish_body(self_ref, lengths_ref, f_ref, z_ref, *rest):
    near_refs, out_ref, all_ref = rest[:-2], rest[-2], rest[-1]
    place = self_ref[0]
    first, length = block_of(lengths_ref, place)
    position = place - first
    for i, near_ref in enumerate(near_refs):
        all_ref[i] = near_ref[...]
    b = []
    for m in range(MOSTT):
        r = all_ref[jnp.clip(MOSTT - 1 + m - position, 0, len(near_refs) - 1)]
        b.append(jnp.where(m < length, r, 0.0))
    total = z_ref[...] + pick(position, apply_inverse(f_ref, b))
    out_ref[...] = total.T


def shift(value, steps):
    count = lax.axis_size(AXES)
    pairs = [(s, s + steps) for s in range(count) if 0 <= s + steps < count]
    return lax.ppermute(value, AXES, pairs)


def exchange(value):
    n, rows, lanes = value.shape
    moved = lax.all_to_all(value.reshape(n * rows, lanes), AXES, 0, 0, tiled=True)
    return moved.reshape(n, rows, lanes)


def body(normal_matrix, right_sides, tile_order, inner_order, block_lengths):
    f32 = jnp.float32
    tile = normal_matrix.shape[0]
    rhs = right_sides.shape[1]
    tiles = tile_order.shape[0]
    per_piece = rhs // (2 * tile // SUB)
    me = lax.axis_index(AXES).astype(jnp.int32).reshape(1)
    smem = pl.BlockSpec(memory_space=pltpu.SMEM)
    vmem = pl.BlockSpec(memory_space=pltpu.VMEM)
    shape = lambda *dims: jax.ShapeDtypeStruct(dims, f32)

    tiles_out, small = pl.pallas_call(
        pack_body,
        out_shape=(shape(tiles, tile, tile), shape(tiles, 2 * SUB, tile)),
        in_specs=[smem, smem, smem, vmem, vmem, vmem],
        out_specs=(vmem, vmem),
        scratch_shapes=[pltpu.VMEM(normal_matrix.shape, f32)],
        name="pack",
    )(me, tile_order, block_lengths, inner_order, normal_matrix, right_sides)

    small_got = exchange(small)
    routed_rows = MOSTT * SUB + -(-MOSTT * per_piece // SUB) * SUB
    routed = pl.pallas_call(
        lambda *refs: route_body(*refs, per_piece=per_piece),
        out_shape=shape(tiles, routed_rows, tile),
        in_specs=[smem, smem, vmem],
        out_specs=vmem,
        scratch_shapes=[pltpu.SMEM((tiles,), jnp.int32)],
        name="route",
    )(tile_order, block_lengths, small_got)
    block_parts = exchange(routed)
    tiles_got = exchange(tiles_out)

    factors, own_sides, z, z_spread = pl.pallas_call(
        lambda *refs: factor_body(*refs, per_piece=per_piece),
        out_shape=(
            shape(2 * MOSTT, tile, tile),
            shape(rhs, tile),
            shape(rhs, tile),
            shape(tiles, rhs, tile),
        ),
        in_specs=[smem, smem, vmem],
        out_specs=(vmem, vmem, vmem, vmem),
        scratch_shapes=[
            pltpu.VMEM((MOSTT, tile, tile), f32),
            pltpu.VMEM((MOSTT, rhs, tile), f32),
        ],
        name="factor",
    )(me, block_lengths, block_parts)

    iterate = exchange(z_spread)
    slab = pl.pallas_call(
        arrange_body,
        out_shape=shape(tiles * tile, tile),
        in_specs=[smem, vmem],
        out_specs=vmem,
        name="arrange",
    )(tile_order, tiles_got)
    residual = pl.pallas_call(
        residual_body,
        out_shape=shape(rhs, tile),
        in_specs=[vmem, vmem, vmem],
        out_specs=vmem,
        name="residual",
    )(slab, iterate, own_sides)
    near = [
        residual if o == 0 else shift(residual, -o) for o in range(1 - MOSTT, MOSTT)
    ]
    solved = pl.pallas_call(
        finish_body,
        out_shape=shape(tile, rhs),
        in_specs=[smem, smem, vmem, vmem] + [vmem] * len(near),
        out_specs=vmem,
        scratch_shapes=[pltpu.VMEM((len(near), rhs, tile), f32)],
        name="finish",
    )(me, block_lengths, factors, z, *near)
    return slab, solved


def solution(mesh):
    placed = (P(AXES, None), P(AXES, None), P(), P(), P())
    return jax.shard_map(
        body,
        mesh=mesh,
        in_specs=placed,
        out_specs=(P(None, AXES), P(AXES, None)),
        check_vma=False,
    )
```

time: 354 us -> 146 us (0.41)
  other arithmetic: 94.5 us -> 0 us
  local copies, waits for them, and re-layouts: 68.8 us -> 4.35 us
  Pallas kernels: 0 us -> 45.6 us
  blocking collectives: 66.2 us -> 35 us
  starting transfers between devices: 44.3 us -> 19.3 us
  waiting for transfers between devices: 63.8 us -> 40.6 us
  matrix products: 10.2 us -> 0 us
  between operations: 5.73 us -> 0.74 us
    another operation x17 -> x0, other arithmetic: 86.7 us -> none  [the longest x11 57 us: body(): factor = jnp.linalg.cholesky(block_matrix)]
    all_gather x1 -> x0, blocking collectives: 66.2 us -> none  [body(): lax.all_gather(iterate, ('gx', 'gy'), axis=0, tiled=True)]
    gather x4 -> x0, local copies, waits for them, and re-layouts: 54.3 us -> none  [the longest x1 23 us: body(): sides_ordered = jnp.take(sides_split, new_to_old, axis=0)]
    pallas_call x0 -> x6, Pallas kernels: none -> 45.6 us  [the longest x1 25.7 us: body(): pl.pallas_call(lambda *refs: factor_body(*refs, per_piece=per_piece), out...]
    all_to_all x0 -> x2, blocking collectives: none -> 35 us  [exchange(): lax.all_to_all(value.reshape(n * rows, lanes), AXES, 0, 0, tiled=True)]
    ppermute x10 -> x4, waiting for transfers between devices: 23.3 us -> 5.55 us  [shift(): return lax.ppermute(value, AXES, pairs)]
    ppermute x10 -> x4, starting transfers between devices: 28.6 us -> 11.7 us  [shift(): return lax.ppermute(value, AXES, pairs)]
    another operation x24 -> x0, matrix products: 8.13 us -> none  [the longest x20 4.47 us: precondition(): solved = jax.scipy.linalg.cho_solve((factor, True), stacked)]
  transfers between devices with their start and end apart: 13 -> 6, of which waited for: 7 -> 4; matrix products, arithmetic and copies ran while one was open for 13% -> 0% of each run, Pallas kernels for 0% -> 20%
where the time goes in v1:
time: 146 us
  Pallas kernels  45.6 us (31%)
  waiting for transfers between devices  40.6 us (28%)
  blocking collectives  35 us (24%)
  starting transfers between devices  19.3 us (13%)
  local copies, waits for them, and re-layouts  4.35 us (3%)
    all_to_all x2, waiting for transfers between devices, exchange(): lax.all_to_all(value.reshape(n * rows, lanes), AXES, 0, 0, tiled=True)  35 us
    all_to_all x2, blocking collectives, exchange(): lax.all_to_all(value.reshape(n * rows, lanes), AXES, 0, 0, tiled=True)  35 us
    pallas_call x1, Pallas kernels, body(): pl.pallas_call(lambda *refs: factor_body(*refs, per_piece=per_piece), out...  25.7 us
    ppermute x4, starting transfers between devices, shift(): return lax.ppermute(value, AXES, pairs)  11.7 us
    pallas_call x1, Pallas kernels, body(): pl.pallas_call(pack_body, out_shape=(shape(tiles, tile, tile), shape(tile...  7.86 us
    all_to_all x2, starting transfers between devices, exchange(): lax.all_to_all(value.reshape(n * rows, lanes), AXES, 0, 0, tiled=True)  7.67 us
    ppermute x4, waiting for transfers between devices, shift(): return lax.ppermute(value, AXES, pairs)  5.55 us
    unnamed x14, local copies, waits for them, and re-layouts  4.35 us
  transfers between devices with their start and end apart: 6, of which 4 were waited for; matrix products, arithmetic and copies ran while one was open for 0% of the time, Pallas kernels for 20%

profile of v1, /device:TPU:2, one launch (start us, length us, event | category | flops | bytes accessed | tf_op | source)
XLA Modules:
  0.0 145.6 jit_solution(8087372272217587160)
XLA Ops:
  0.6 1.4 copy.7.sides_ref
  2.1 7.9 %pack.1 = (f32[32,128,128]{2,1,0:T(8,128)}, f32[32,16,128]{2,1,0:T(8,128)}) custom-call(s32[1]{0:T(128)} %bitcast.self_ref.refs_0_, s32[32]{0:T(128)} %refs_0_.1, s32[16]{0:T(128)} %lengths_ref.3, s32[32,128]{1,0:T(8,128)} %inner_ref.1, f32[128,4096]{1,0:T(8,128)} %slab_ref.1, f32[128,32]{1,0:T(8,128)} %copy.7.sides_ref), custom_call_target="tpu_custom_call" | custom-call | tf_op jit(solution)/shard_map/pack/pallas_call | solution.py:315
  9.9 15.5 %all_to_all.24.refs_2_ = f32[32,16,128]{2,1,0:T(8,128)} all-to-all(f32[32,16,128]{2,1,0:T(8,128)} %get-tuple-element.9), channel_id=1, replica_groups=mesh['gx'=4,'gy'=8] {'gx','gy'}, dimensions={0} | all-to-all | bytes 524288 | tf_op jit(solution)/shard_map/all_to_all | solution.py:300
  25.4 2.3 %route.1 = f32[32,32,128]{2,1,0:T(8,128)} custom-call(s32[32]{0:T(128)} %refs_0_.1, s32[16]{0:T(128)} %lengths_ref.3, f32[32,16,128]{2,1,0:T(8,128)} %all_to_all.24.refs_2_), custom_call_target="tpu_custom_call" | custom-call | tf_op jit(solution)/shard_map/route/pallas_call | solution.py:326
  27.7 19.5 %all_to_all.25.refs_2_ = f32[32,32,128]{2,1,0:T(8,128)} all-to-all(f32[32,32,128]{2,1,0:T(8,128)} %route.1), channel_id=1, replica_groups=mesh['gx'=4,'gy'=8] {'gx','gy'}, dimensions={0} | all-to-all | bytes 1048576 | tf_op jit(solution)/shard_map/all_to_all | solution.py:300
  47.2 3.8 %all-to-all-start = ((f32[32,128,128]{2,1,0:T(8,128)}), f32[32,128,128]{2,1,0:T(8,128)S(1)}, u32[]{:S(2)}, u32[]{:S(2)}) async-start(f32[32,128,128]{2,1,0:T(8,128)} %get-tuple-element.8), calls=%async_computation | async-start | bytes 4194304 | tf_op jit(solution)/shard_map/all_to_all | solution.py:300
  51.0 25.7 %factor.1 = (f32[6,128,128]{2,1,0:T(8,128)}, f32[32,128]{1,0:T(8,128)}, f32[32,128]{1,0:T(8,128)}, f32[32,32,128]{2,1,0:T(8,128)}) custom-call(s32[1]{0:T(128)} %bitcast.self_ref.refs_0_, s32[16]{0:T(128)} %lengths_ref.3, f32[32,32,128]{2,1,0:T(8,128)} %all_to_all.25.refs_2_), custom_call_target="tpu_custom_call" | custom-call | tf_op jit(solution)/shard_map/factor/pallas_call | solution.py:337
  76.8 23.1 %all-to-all-done.got_ref = f32[32,128,128]{2,1,0:T(8,128)S(1)} async-done(((f32[32,128,128]{2,1,0:T(8,128)}), f32[32,128,128]{2,1,0:T(8,128)S(1)}, u32[]{:S(2)}, u32[]{:S(2)}) %all-to-all-start) | async-done | bytes 2097184 | tf_op jit(solution)/shard_map/all_to_all | solution.py:300
  99.9 3.9 %all-to-all-start.3 = ((f32[32,32,128]{2,1,0:T(8,128)}), f32[32,32,128]{2,1,0:T(8,128)S(1)}, u32[]{:S(2)}, u32[]{:S(2)}) async-start(f32[32,32,128]{2,1,0:T(8,128)} %get-tuple-element.12), calls=%async_computation.3 | async-start | bytes 1048576 | tf_op jit(solution)/shard_map/all_to_all | solution.py:300
  103.8 3.2 %arrange.1.slab_ref = f32[4096,128]{1,0:T(8,128)} custom-call(s32[32]{0:T(128)} %refs_0_.1, f32[32,128,128]{2,1,0:T(8,128)} %copy-done), custom_call_target="tpu_custom_call" | custom-call | tf_op jit(solution)/shard_map/arrange/pallas_call | solution.py:355
  107.0 11.9 %all-to-all-done.3.iterate_ref = f32[32,32,128]{2,1,0:T(8,128)S(1)} async-done(((f32[32,32,128]{2,1,0:T(8,128)}), f32[32,32,128]{2,1,0:T(8,128)S(1)}, u32[]{:S(2)}, u32[]{:S(2)}) %all-to-all-start.3) | async-done | bytes 524320 | tf_op jit(solution)/shard_map/all_to_all | solution.py:300
  118.9 0.8 copy-done.1
  119.7 3.4 %residual.1.rest_2_ = f32[32,128]{1,0:T(8,128)} custom-call(f32[4096,128]{1,0:T(8,128)} %arrange.1.slab_ref, f32[32,32,128]{2,1,0:T(8,128)} %copy-done.1, f32[32,128]{1,0:T(8,128)} %get-tuple-element.13.b_ref), custom_call_target="tpu_custom_call" | custom-call | tf_op jit(solution)/shard_map/residual/pallas_call | solution.py:362
  123.0 3.5 %collective-permute-start.3 = (f32[32,128]{1,0:T(8,128)}, f32[32,128]{1,0:T(8,128)S(1)}, u32[]{:S(2)}, u32[]{:S(2)}) collective-permute-start(f32[32,128]{1,0:T(8,128)} %residual.1.rest_2_), channel_id=1, source_target_pairs={{2,0},{3,1},{4,2},{5,3},{6,4},{7,5},{8,6},{9,7},{10,8},{11,9},{12,... | collective-permute-start | bytes 49160 | tf_op jit(solution)/shard_map/ppermute | solution.py:295
  126.5 2.6 %collective-permute-start.2 = (f32[32,128]{1,0:T(8,128)}, f32[32,128]{1,0:T(8,128)S(1)}, u32[]{:S(2)}, u32[]{:S(2)}) collective-permute-start(f32[32,128]{1,0:T(8,128)} %residual.1.rest_2_), channel_id=1, source_target_pairs={{1,0},{2,1},{3,2},{4,3},{5,4},{6,5},{7,6},{8,7},{9,8},{10,9},{11,1... | collective-permute-start | bytes 49160 | tf_op jit(solution)/shard_map/ppermute | solution.py:295
  129.1 3.3 %collective-permute-start.1 = (f32[32,128]{1,0:T(8,128)}, f32[32,128]{1,0:T(8,128)S(1)}, u32[]{:S(2)}, u32[]{:S(2)}) collective-permute-start(f32[32,128]{1,0:T(8,128)} %residual.1.rest_2_), channel_id=1, source_target_pairs={{0,1},{1,2},{2,3},{3,4},{4,5},{5,6},{6,7},{7,8},{8,9},{9,10},{10,1... | collective-permute-start | bytes 49160 | tf_op jit(solution)/shard_map/ppermute | solution.py:295
  132.4 2.4 %collective-permute-start = (f32[32,128]{1,0:T(8,128)}, f32[32,128]{1,0:T(8,128)S(1)}, u32[]{:S(2)}, u32[]{:S(2)}) collective-permute-start(f32[32,128]{1,0:T(8,128)} %residual.1.rest_2_), channel_id=1, source_target_pairs={{0,2},{1,3},{2,4},{3,5},{4,6},{5,7},{6,8},{7,9},{8,10},{9,11},{10,... | collective-permute-start | bytes 49160 | tf_op jit(solution)/shard_map/ppermute | solution.py:295
  134.8 0.0 collective-permute-done.3.rest_4_
  134.8 0.0 collective-permute-done.2.rest_3_
  134.8 3.2 %collective-permute-done.1.rest_1_ = f32[32,128]{1,0:T(8,128)S(1)} collective-permute-done((f32[32,128]{1,0:T(8,128)}, f32[32,128]{1,0:T(8,128)S(1)}, u32[]{:S(2)}, u32[]{:S(2)}) %collective-permute-start.1) | collective-permute-done | bytes 16416 | tf_op jit(solution)/shard_map/ppermute | solution.py:295
  138.0 2.3 %collective-permute-done.rest_0_ = f32[32,128]{1,0:T(8,128)S(1)} collective-permute-done((f32[32,128]{1,0:T(8,128)}, f32[32,128]{1,0:T(8,128)S(1)}, u32[]{:S(2)}, u32[]{:S(2)}) %collective-permute-start) | collective-permute-done | bytes 16416 | tf_op jit(solution)/shard_map/ppermute | solution.py:295
  140.3 0.6 copy-done.5
  140.9 3.1 %finish.1 = f32[128,32]{1,0:T(8,128)} custom-call(s32[1]{0:T(128)} %bitcast.self_ref.refs_0_, s32[16]{0:T(128)} %lengths_ref.3, f32[6,128,128]{2,1,0:T(8,128)} %get-tuple-element.10.f_ref, f32[32,128]{1,0:T(8,128)} %get-tuple-element.11.z_ref, f32[32,128]{1,0:T(8,128)} %copy-done.5, f32[32,128]{1,0:T(8,128)} %copy-done.4, f32[32,128]{1,0:T(8,128)} %residual.1.rest_2_, ...), custom_call_target="tpu_custom_call" | custom-call | tf_op jit(solution)/shard_map/finish/pallas_call | solution.py:372
  144.1 1.5 %copy.8 = f32[128,32]{0,1:T(8,128)} copy(f32[128,32]{1,0:T(8,128)} %finish.1) | data formatting | bytes 32768
  (10 shorter events, 0.0 us)
Async XLA Ops:
  47.2 52.7 %all-to-all-start = ((f32[32,128,128]{2,1,0:T(8,128)}), f32[32,128,128]{2,1,0:T(8,128)S(1)}, u32[]{:S(2)}, u32[]{:S(2)}) async-start(f32[32,128,128]{2,1,0:T(8,128)} %get-tuple-element.8), calls=%async_computation | async-start | bytes 4194304 | tf_op jit(solution)/shard_map/all_to_all | solution.py:300
  99.9 3.9 %copy-start = (f32[32,128,128]{2,1,0:T(8,128)}, f32[32,128,128]{2,1,0:T(8,128)S(1)}, u32[]{:S(2)}) copy-start(f32[32,128,128]{2,1,0:T(8,128)S(1)} %all-to-all-done.got_ref) | copy-start | bytes 6291460
  99.9 19.0 %all-to-all-start.3 = ((f32[32,32,128]{2,1,0:T(8,128)}), f32[32,32,128]{2,1,0:T(8,128)S(1)}, u32[]{:S(2)}, u32[]{:S(2)}) async-start(f32[32,32,128]{2,1,0:T(8,128)} %get-tuple-element.12), calls=%async_computation.3 | async-start | bytes 1048576 | tf_op jit(solution)/shard_map/all_to_all | solution.py:300
  118.9 0.8 copy-start.1
  123.0 11.7 %collective-permute-start.3 = (f32[32,128]{1,0:T(8,128)}, f32[32,128]{1,0:T(8,128)S(1)}, u32[]{:S(2)}, u32[]{:S(2)}) collective-permute-start(f32[32,128]{1,0:T(8,128)} %residual.1.rest_2_), channel_id=1, source_target_pairs={{2,0},{3,1},{4,2},{5,3},{6,4},{7,5},{8,6},{9,7},{10,8},{11,9},{12,... | collective-permute-start | bytes 49160 | tf_op jit(solution)/shard_map/ppermute | solution.py:295
  126.5 8.3 %collective-permute-start.2 = (f32[32,128]{1,0:T(8,128)}, f32[32,128]{1,0:T(8,128)S(1)}, u32[]{:S(2)}, u32[]{:S(2)}) collective-permute-start(f32[32,128]{1,0:T(8,128)} %residual.1.rest_2_), channel_id=1, source_target_pairs={{1,0},{2,1},{3,2},{4,3},{5,4},{6,5},{7,6},{8,7},{9,8},{10,9},{11,1... | collective-permute-start | bytes 49160 | tf_op jit(solution)/shard_map/ppermute | solution.py:295
  129.1 8.9 %collective-permute-start.1 = (f32[32,128]{1,0:T(8,128)}, f32[32,128]{1,0:T(8,128)S(1)}, u32[]{:S(2)}, u32[]{:S(2)}) collective-permute-start(f32[32,128]{1,0:T(8,128)} %residual.1.rest_2_), channel_id=1, source_target_pairs={{0,1},{1,2},{2,3},{3,4},{4,5},{5,6},{6,7},{7,8},{8,9},{9,10},{10,1... | collective-permute-start | bytes 49160 | tf_op jit(solution)/shard_map/ppermute | solution.py:295
  132.4 8.0 %collective-permute-start = (f32[32,128]{1,0:T(8,128)}, f32[32,128]{1,0:T(8,128)S(1)}, u32[]{:S(2)}, u32[]{:S(2)}) collective-permute-start(f32[32,128]{1,0:T(8,128)} %residual.1.rest_2_), channel_id=1, source_target_pairs={{0,2},{1,3},{2,4},{3,5},{4,6},{5,7},{6,8},{7,9},{8,10},{9,11},{10,... | collective-permute-start | bytes 49160 | tf_op jit(solution)/shard_map/ppermute | solution.py:295
  134.8 5.6 %copy-start.2 = (f32[32,128]{1,0:T(8,128)}, f32[32,128]{1,0:T(8,128)S(1)}, u32[]{:S(2)}) copy-start(f32[32,128]{1,0:T(8,128)S(1)} %collective-permute-done.3.rest_4_) | copy-start | bytes 49156
  134.8 5.6 %copy-start.3 = (f32[32,128]{1,0:T(8,128)}, f32[32,128]{1,0:T(8,128)S(1)}, u32[]{:S(2)}) copy-start(f32[32,128]{1,0:T(8,128)S(1)} %collective-permute-done.2.rest_3_) | copy-start | bytes 49156
  138.0 2.3 %copy-start.4 = (f32[32,128]{1,0:T(8,128)}, f32[32,128]{1,0:T(8,128)S(1)}, u32[]{:S(2)}) copy-start(f32[32,128]{1,0:T(8,128)S(1)} %collective-permute-done.1.rest_1_) | copy-start | bytes 49156
  140.3 0.6 copy-start.5

commit v2 on v1

v2 whole, which is shorter than its diff:
```python
import jax
import jax.numpy as jnp
from jax import lax
from jax.experimental import pallas as pl
from jax.experimental.pallas import tpu as pltpu
from jax.sharding import PartitionSpec as P


MOSTT = 3
AXES = ("gx", "gy")
SUB = 8
HIGHEST = lax.Precision.HIGHEST


def dot(a, b, contract=((1,), (0,))):
    return lax.dot_general(
        a, b, (contract, ((), ())), precision=HIGHEST, preferred_element_type=jnp.float32
    )


def dot_t(a, b):
    return dot(a, b, ((1,), (1,)))


def one_pass(a, b):
    return lax.dot_general(a, b, (((1,), (0,)), ((), ())), preferred_element_type=jnp.float32)


def place_of_tile(order_ref, tiles, old_tile):
    def step(t, found):
        return jnp.where(order_ref[t] == old_tile, t, found)

    return lax.fori_loop(0, tiles, step, jnp.int32(0))


def block_of(lengths_ref, place):
    def step(e, carry):
        start, first, length = carry
        here = (start <= place) & (place < start + lengths_ref[e])
        first = jnp.where(here, start, first)
        length = jnp.where(here, lengths_ref[e], length)
        return start + lengths_ref[e], first, length

    zero = jnp.int32(0)
    _, first, length = lax.fori_loop(0, lengths_ref.shape[0], step, (zero, zero, zero + 1))
    return first, length


def split_rows(hot, x):
    high = x.astype(jnp.bfloat16)
    rest = x - high.astype(jnp.float32)
    middle = rest.astype(jnp.bfloat16)
    low = (rest - middle.astype(jnp.float32)).astype(jnp.bfloat16)
    return (one_pass(hot, low) + one_pass(hot, middle)) + one_pass(hot, high)


def row_choice(inner_row, tile):
    hot = jnp.where(lax.broadcasted_iota(jnp.int32, (tile, tile), 0) == inner_row, 1.0, 0.0)
    return hot.T.astype(jnp.bfloat16)


def sides_fit(tile, rhs):
    return 4 * rhs == tile


def near_body(self_ref, order_ref, lengths_ref, inner_ref, sides_ref, slab_ref, small_ref, near_ref, sems):
    tile = slab_ref.shape[0]
    tiles = order_ref.shape[0]
    rhs = sides_ref.shape[0]
    me = self_ref[0]
    place = place_of_tile(order_ref, tiles, me)
    first, _ = block_of(lengths_ref, place)
    position = place - first
    after = jnp.where(position == MOSTT - 1, 0, position + 1)
    beside = jnp.minimum(first + after, tiles - 1)
    places = (place, beside)
    copies = []
    for i, t in enumerate(places):
        at = pl.ds(pl.multiple_of(order_ref[t] * tile, tile), tile)
        copies.append(pltpu.make_async_copy(slab_ref.at[:, at], near_ref.at[i], sems.at[i]))
        copies[-1].start()
    own_inner = inner_ref[pl.ds(place, 1), :]
    row_hot = row_choice(own_inner, tile)
    turned = jnp.take_along_axis(
        sides_ref[...], jnp.broadcast_to(own_inner, (rhs, tile)), axis=1
    )
    pieces = 2 * tile // SUB
    rows = small_ref.shape[0] // tiles
    half = tile // 2
    lane = lax.broadcasted_iota(jnp.int32, (SUB, tile), 1)
    if small_ref.shape[0] > pieces * rows:
        small_ref[pieces * rows :, :] = jnp.zeros((small_ref.shape[0] - pieces * rows, tile), jnp.float32)
    for i, t in enumerate(places):
        copies[i].wait()
        moved = split_rows(row_hot, near_ref[i])
        chosen = jnp.broadcast_to(inner_ref[pl.ds(t, 1), :], (tile, tile))
        moved = jnp.take_along_axis(moved, chosen, axis=1)
        if i == 0 and sides_fit(tile, rhs):
            extra = jnp.concatenate([turned, pltpu.roll(turned, half, 1)], axis=0)
        for k in range(pieces // 2):
            chunk = moved[k * SUB : (k + 1) * SUB, :]
            if i == 0 and sides_fit(tile, rhs) and k * SUB >= half:
                chunk = jnp.where(lane < half, extra[k * SUB - half : (k + 1) * SUB - half, :], chunk)
            at = (i * (pieces // 2) + k) * rows
            small_ref[at : at + SUB, :] = chunk
    if not sides_fit(tile, rhs):
        per_piece = rhs // pieces
        for k in range(pieces):
            at = k * rows + SUB
            small_ref[at : at + SUB, :] = jnp.zeros((SUB, tile), jnp.float32)
            small_ref[at : at + per_piece, :] = turned[k * per_piece : (k + 1) * per_piece, :]


def pack_body(self_ref, order_ref, inner_ref, slab_ref, send_ref, rows_ref):
    tile = slab_ref.shape[0]
    tiles = order_ref.shape[0]
    place = place_of_tile(order_ref, tiles, self_ref[0])
    row_hot = row_choice(inner_ref[pl.ds(place, 1), :], tile)
    width = slab_ref.shape[1]
    step = min(width, 8 * tile)

    def order_rows(c, _):
        at = pl.ds(pl.multiple_of(c * step, step), step)
        rows_ref[:, at] = split_rows(row_hot, slab_ref[:, at])
        return 0

    lax.fori_loop(0, width // step, order_rows, 0)

    def order_columns(t, _):
        at = pl.ds(pl.multiple_of(order_ref[t] * tile, tile), tile)
        chosen = jnp.broadcast_to(inner_ref[pl.ds(t, 1), :], (SUB, tile))
        for g in range(tile // SUB):
            x = rows_ref[g * SUB : (g + 1) * SUB, at]
            send_ref[t, g * SUB : (g + 1) * SUB, :] = jnp.take_along_axis(x, chosen, axis=1)
        return 0

    lax.fori_loop(0, tiles, order_columns, 0)


def route_body(order_ref, lengths_ref, got_ref, send_ref, first_ref, *, per_piece):
    tiles = order_ref.shape[0]

    def block(e, start):
        for j in range(MOSTT):
            @pl.when(j < lengths_ref[e])
            def _():
                first_ref[start + j] = start
        return start + lengths_ref[e]

    lax.fori_loop(0, lengths_ref.shape[0], block, jnp.int32(0))
    spare = send_ref.shape[1] - MOSTT * SUB

    def fill(d, _):
        if spare:
            send_ref[d, MOSTT * SUB :, :] = jnp.zeros((spare, send_ref.shape[2]), jnp.float32)
        for m in range(MOSTT):
            source = order_ref[jnp.minimum(first_ref[d] + m, tiles - 1)]
            send_ref[d, m * SUB : (m + 1) * SUB, :] = got_ref[source, 0:SUB, :]
            if spare:
                at = MOSTT * SUB + m * per_piece
                send_ref[d, at : at + per_piece, :] = got_ref[source, SUB : SUB + per_piece, :]
        return 0

    lax.fori_loop(0, tiles, fill, 0)


def sweep(s):
    for k in range(SUB):
        inverse = pltpu.reciprocal(s[k][k], approx=False)
        column = [s[max(i, k)][min(i, k)] for i in range(SUB)]
        scaled = [column[i] * inverse for i in range(SUB)]
        for i in range(SUB):
            for j in range(i + 1):
                if i != k and j != k:
                    s[i][j] = s[i][j] - scaled[i] * column[j]
        for i in range(SUB):
            if i != k:
                s[max(i, k)][min(i, k)] = scaled[i]
        s[k][k] = -inverse
    return s


def invert_in_place(m_ref):
    size = m_ref.shape[0]
    lane = lax.broadcasted_iota(jnp.int32, (SUB, size), 1)
    sub = lax.broadcasted_iota(jnp.int32, (SUB, size), 0)

    def panel(p, _):
        row = pl.multiple_of(p * SUB, SUB)
        rows = m_ref[pl.ds(row, SUB), :]
        inside = (lane >= row) & (lane < row + SUB)
        at = [jnp.full((SUB, size), row + j, jnp.int32) for j in range(SUB)]
        columns = [jnp.take_along_axis(rows, at[j], axis=1) for j in range(SUB)]
        s = [
            [jnp.broadcast_to(columns[j][i : i + 1, :], (SUB, size)) for j in range(i + 1)]
            for i in range(SUB)
        ]
        s = sweep(s)
        spread = [
            jnp.where(
                inside,
                jnp.where(lane == row + j, 1.0, 0.0),
                jnp.broadcast_to(rows[j : j + 1, :], (SUB, size)),
            )
            for j in range(SUB)
        ]
        update = []
        for i in range(SUB):
            total = s[i][0] * spread[0]
            for j in range(1, SUB):
                total = total + s[max(i, j)][min(i, j)] * spread[j]
            update.append(total)
        new = -update[0]
        for i in range(1, SUB):
            new = jnp.where(sub == i, -update[i], new)
        for g in range(size // SUB):
            here = m_ref[g * SUB : (g + 1) * SUB, :]
            total = jnp.where(inside, 0.0, here)
            for j in range(SUB):
                total = total + jnp.take_along_axis(here, at[j], axis=1) * update[j]
            m_ref[g * SUB : (g + 1) * SUB, :] = total
        m_ref[pl.ds(row, SUB), :] = new
        return 0

    lax.fori_loop(0, size // SUB, panel, 0)


def block_inverse(f_ref, w01, w02, w12):
    e0, e1, e2 = f_ref[0], f_ref[1], f_ref[2]
    v12 = -dot(w12, e2)
    v11 = e1 - dot_t(v12, w12)
    v02 = -dot(w01, v12) - dot(w02, e2)
    v01 = -dot(w01, v11) - dot_t(w02, v12)
    v00 = e0 - dot_t(v01, w01) - dot_t(v02, w02)
    return (v00, v01, v02), (v01.T, v11, v12), (v02.T, v12.T, e2)


def apply_rows(v_ref, b):
    return dot_t(jnp.concatenate(b, axis=1), v_ref[...])


def pick(position, values):
    chosen = values[0]
    for m in range(1, len(values)):
        chosen = jnp.where(position == m, values[m], chosen)
    return chosen


def factor_body(self_ref, lengths_ref, got_ref, v_ref, b_ref, z_ref, f_ref, o_ref, bs_ref, *, per_piece):
    tile = got_ref.shape[2]
    rhs = b_ref.shape[0]
    pieces = 2 * tile // SUB
    half = tile // 2
    first, length = block_of(lengths_ref, self_ref[0])
    position = self_ref[0] - first
    row = lax.broadcasted_iota(jnp.int32, (tile, tile), 0)
    lane = lax.broadcasted_iota(jnp.int32, (tile, tile), 1)
    for m in range(MOSTT):
        pair_inside = m + 1 < length if m < MOSTT - 1 else m < length
        for k in range(pieces // 2):
            at = slice(k * SUB, (k + 1) * SUB)
            f_ref[m, at, :] = got_ref[k, m * SUB : (m + 1) * SUB, :]
            beside = got_ref[k + pieces // 2, m * SUB : (m + 1) * SUB, :]
            o_ref[m, at, :] = jnp.where(pair_inside, beside, 0.0)
        own = f_ref[m]
        if sides_fit(tile, rhs):
            low = own[half : half + rhs, :]
            high = pltpu.roll(own[half + rhs :, :], half, 1)
            side = jnp.where(lane[:rhs, :] < half, low, high)
            own = jnp.where((row >= half) & (lane < half), own.T, own)
            bs_ref[m] = jnp.where(m < length, side, 0.0)
        else:
            for k in range(pieces):
                start = MOSTT * SUB + m * per_piece
                part = got_ref[k, start : start + per_piece, :]
                bs_ref[m, k * per_piece : (k + 1) * per_piece, :] = jnp.where(m < length, part, 0.0)
        f_ref[m] = jnp.where(m < length, own, jnp.where(row == lane, 1.0, 0.0))
    a01 = o_ref[0]
    a12 = o_ref[1]
    a20 = o_ref[2]
    a10 = a01.T
    invert_in_place(f_ref.at[0])
    w01 = dot(f_ref[0], a01)
    w02 = dot_t(f_ref[0], a20)
    f_ref[1] = f_ref[1] - dot(a10, w01)
    s12 = a12 - dot(a10, w02)
    invert_in_place(f_ref.at[1])
    w12 = dot(f_ref[1], s12)
    f_ref[2] = f_ref[2] - dot(a20, w02) - dot(s12.T, w12)
    invert_in_place(f_ref.at[2])
    rows = block_inverse(f_ref, w01, w02, w12)
    for m in range(MOSTT):
        v_ref[:, m * tile : (m + 1) * tile] = pick(position, [rows[p][m] for p in range(MOSTT)])
    b = [bs_ref[m] for m in range(MOSTT)]
    b_ref[...] = pick(position, b)
    z_ref[...] = apply_rows(v_ref, b)


def arrange_body(order_ref, got_ref, slab_ref):
    tiles = order_ref.shape[0]
    tile = got_ref.shape[1]

    def move(t, _):
        slab_ref[pl.ds(pl.multiple_of(t * tile, tile), tile), :] = got_ref[order_ref[t]]
        return 0

    lax.fori_loop(0, tiles, move, 0)


def residual_body(self_ref, order_ref, got_ref, b_ref, *rest, flips):
    part_refs, r_ref, x_ref = rest[:-2], rest[-2], rest[-1]
    _, tile = b_ref.shape
    tiles = order_ref.shape[0]
    me = self_ref[0]
    j = 0
    for part_ref in part_refs:
        for i in range(part_ref.shape[0]):
            at = pl.multiple_of(order_ref[me ^ flips[j]] * tile, tile)
            x_ref[:, pl.ds(at, tile)] = part_ref[i]
            j += 1
    group = 8
    total = b_ref[...]
    for c in range(tiles // group):
        x = x_ref[:, c * group * tile : (c + 1) * group * tile]
        g = got_ref[c * group : (c + 1) * group].reshape(group * tile, tile)
        total = total - dot(x, g)
    r_ref[...] = total


def finish_body(self_ref, lengths_ref, v_ref, z_ref, *rest):
    near_refs, out_ref, all_ref = rest[:-2], rest[-2], rest[-1]
    place = self_ref[0]
    first, length = block_of(lengths_ref, place)
    position = place - first
    for i, near_ref in enumerate(near_refs):
        all_ref[i] = near_ref[...]
    b = []
    for m in range(MOSTT):
        r = all_ref[jnp.clip(MOSTT - 1 + m - position, 0, len(near_refs) - 1)]
        b.append(jnp.where(m < length, r, 0.0))
    out_ref[...] = z_ref[...] + apply_rows(v_ref, b)


def shift(value, steps):
    count = lax.axis_size(AXES)
    return lax.ppermute(value, AXES, [(s, (s + steps) % count) for s in range(count)])


def exchange(value, rows):
    lanes = value.shape[-1]
    moved = lax.all_to_all(value.reshape(-1, lanes), AXES, 0, 0, tiled=True)
    return moved.reshape(-1, rows, lanes)


def swap(value, bit):
    count = lax.axis_size(AXES)
    return lax.ppermute(value, AXES, [(s, s ^ bit) for s in range(count)])


def spread(value):
    count_x, count_y = lax.axis_size("gx"), lax.axis_size("gy")
    assert count_x & (count_x - 1) == 0 and count_y & (count_y - 1) == 0
    low = 1 << ((count_y.bit_length() - 1) // 2)
    held, flips = value[None], [0]
    bits = [count_y << i for i in range(1, count_x.bit_length() - 1)]
    bits += [1 << i for i in range(low.bit_length() - 1)]
    for bit in bits:
        held = jnp.concatenate([held, swap(held, bit)], axis=0)
        flips += [f ^ bit for f in flips]
    across = [low * i for i in range(1, count_y // low)]
    parts = [held] + [swap(held, bit) for bit in across]
    held = jnp.concatenate(parts, axis=0)
    flips += [f ^ bit for bit in across for f in flips]
    if count_x > 1:
        parts = [held, swap(held, count_y)]
        flips += [f ^ count_y for f in flips]
    else:
        parts = [held]
    return parts, tuple(flips)


def body(normal_matrix, right_sides, tile_order, inner_order, block_lengths):
    f32 = jnp.float32
    tile = normal_matrix.shape[0]
    rhs = right_sides.shape[1]
    tiles = tile_order.shape[0]
    per_piece = rhs // (2 * tile // SUB)
    fit = sides_fit(tile, rhs)
    me = lax.axis_index(AXES).astype(jnp.int32).reshape(1)
    smem = pl.BlockSpec(memory_space=pltpu.SMEM)
    vmem = pl.BlockSpec(memory_space=pltpu.VMEM)
    hbm = pl.BlockSpec(memory_space=pl.ANY)
    shape = lambda *dims: jax.ShapeDtypeStruct(dims, f32)

    small_rows = SUB if fit else 2 * SUB
    small = pl.pallas_call(
        near_body,
        out_shape=shape(tiles * small_rows, tile),
        in_specs=[smem, smem, smem, vmem, vmem, hbm],
        out_specs=vmem,
        scratch_shapes=[pltpu.VMEM((2, tile, tile), f32), pltpu.SemaphoreType.DMA((2,))],
        name="near",
    )(me, tile_order, block_lengths, inner_order, right_sides.T, normal_matrix)
    small_got = exchange(small, small_rows)
    tiles_out = pl.pallas_call(
        pack_body,
        out_shape=shape(tiles, tile, tile),
        in_specs=[smem, smem, vmem, vmem],
        out_specs=vmem,
        scratch_shapes=[pltpu.VMEM(normal_matrix.shape, f32)],
        name="pack",
    )(me, tile_order, inner_order, normal_matrix)
    routed_rows = MOSTT * SUB + (0 if fit else -(-MOSTT * per_piece // SUB) * SUB)
    routed = pl.pallas_call(
        lambda *refs: route_body(*refs, per_piece=per_piece),
        out_shape=shape(tiles, routed_rows, tile),
        in_specs=[smem, smem, vmem],
        out_specs=vmem,
        scratch_shapes=[pltpu.SMEM((tiles,), jnp.int32)],
        name="route",
    )(tile_order, block_lengths, small_got)
    block_parts = exchange(routed, routed_rows)
    tiles_got = exchange(tiles_out, tile)

    inverse_rows, own_sides, z = pl.pallas_call(
        lambda *refs: factor_body(*refs, per_piece=per_piece),
        out_shape=(shape(tile, MOSTT * tile), shape(rhs, tile), shape(rhs, tile)),
        in_specs=[smem, smem, vmem],
        out_specs=(vmem, vmem, vmem),
        scratch_shapes=[
            pltpu.VMEM((MOSTT, tile, tile), f32),
            pltpu.VMEM((MOSTT, tile, tile), f32),
            pltpu.VMEM((MOSTT, rhs, tile), f32),
        ],
        name="factor",
    )(me, block_lengths, block_parts)

    iterate, flips = spread(z)
    slab = pl.pallas_call(
        arrange_body,
        out_shape=shape(tiles * tile, tile),
        in_specs=[smem, vmem],
        out_specs=vmem,
        name="arrange",
    )(tile_order, tiles_got)
    residual = pl.pallas_call(
        lambda *refs: residual_body(*refs, flips=flips),
        out_shape=shape(rhs, tile),
        in_specs=[smem, smem, vmem, vmem] + [vmem] * len(iterate),
        out_specs=vmem,
        scratch_shapes=[pltpu.VMEM((rhs, tiles * tile), f32)],
        name="residual",
    )(me, tile_order, tiles_got, own_sides, *iterate)
    near = [
        residual if o == 0 else shift(residual, -o) for o in range(1 - MOSTT, MOSTT)
    ]
    solved = pl.pallas_call(
        finish_body,
        out_shape=shape(rhs, tile),
        in_specs=[smem, smem, vmem, vmem] + [vmem] * len(near),
        out_specs=vmem,
        scratch_shapes=[pltpu.VMEM((len(near), rhs, tile), f32)],
        name="finish",
    )(me, block_lengths, inverse_rows, z, *near)
    return slab, solved.T


def solution(mesh):
    placed = (P(AXES, None), P(AXES, None), P(), P(), P())
    return jax.shard_map(
        body,
        mesh=mesh,
        in_specs=placed,
        out_specs=(P(None, AXES), P(AXES, None)),
        check_vma=False,
    )
```

time: 146 us -> 114 us (0.78)
  the two profiles are of different devices: /device:TPU:2 before, /device:TPU:0 now
where the time goes in v2:
time: 114 us
  Pallas kernels  47.5 us (42%)
  waiting for transfers between devices  24.2 us (21%)
  starting transfers between devices  21.6 us (19%)
  blocking collectives  15.3 us (13%)
  local copies, waits for them, and re-layouts  2.82 us (2%)
  other arithmetic  1.44 us (1%)
    pallas_call x1, Pallas kernels, body(): pl.pallas_call(lambda *refs: factor_body(*refs, per_piece=per_piece), out...  25.8 us
    ppermute x6, waiting for transfers between devices, swap(): return lax.ppermute(value, AXES, [(s, s ^ bit) for s in range(count)])  16.5 us
    all_to_all x1, blocking collectives, exchange(): moved = lax.all_to_all(value.reshape(-1, lanes), AXES, 0, 0, tiled=True)  15.3 us
    ppermute x6, starting transfers between devices, swap(): return lax.ppermute(value, AXES, [(s, s ^ bit) for s in range(count)])  11.3 us
    pallas_call x1, Pallas kernels, body(): pl.pallas_call(pack_body, out_shape=shape(tiles, tile, tile), in_specs=[s...  7.68 us
    all_to_all x2, waiting for transfers between devices, exchange(): moved = lax.all_to_all(value.reshape(-1, lanes), AXES, 0, 0, tiled=True)  5.74 us
    all_to_all x2, starting transfers between devices, exchange(): moved = lax.all_to_all(value.reshape(-1, lanes), AXES, 0, 0, tiled=True)  5.32 us
    ppermute x4, starting transfers between devices, shift(): lax.ppermute(value, AXES, [(s, (s + steps) % count) for s in range(count)])  5.01 us
  transfers between devices with their start and end apart: 12, of which 8 were waited for; matrix products, arithmetic and copies ran while one was open for 2% of the time, Pallas kernels for 32%

profile of v2, /device:TPU:0, one launch (start us, length us, event | category | flops | bytes accessed | tf_op | source)
XLA Modules:
  0.0 113.6 jit_solution(10082359106485628313)
XLA Ops:
  0.6 3.2 %near.1 = f32[256,128]{1,0:T(8,128)} custom-call(s32[1]{0:T(128)} %bitcast.self_ref.refs_0_, s32[32]{0:T(128)} %refs_1_.5, s32[16]{0:T(128)} %lengths_ref.3, s32[32,128]{1,0:T(8,128)} %inner_ref.3, f32[32,128]{1,0:T(8,128)} %bitcast.10, f32[128,4096]{1,0:T(8,128)} %slab_ref.3), custom_call_target="tpu_custom_call" | custom-call | tf_op jit(solution)/shard_map/near/pallas_call | solution.py:396
  3.9 15.3 %all_to_all.21.refs_2_ = f32[32,8,128]{2,1,0:T(8,128)} all-to-all(f32[32,8,128]{2,1,0:T(8,128)} %bitcast.6), channel_id=1, replica_groups=mesh['gx'=4,'gy'=8] {'gx','gy'}, dimensions={0} | all-to-all | bytes 262144 | tf_op jit(solution)/shard_map/all_to_all | solution.py:351
  19.1 2.2 %route.1 = f32[32,24,128]{2,1,0:T(8,128)} custom-call(s32[32]{0:T(128)} %refs_1_.5, s32[16]{0:T(128)} %lengths_ref.3, f32[32,8,128]{2,1,0:T(8,128)} %all_to_all.21.refs_2_), custom_call_target="tpu_custom_call" | custom-call | tf_op jit(solution)/shard_map/route/pallas_call | solution.py:414
  21.3 2.6 %all-to-all-start.2 = ((f32[32,24,128]{2,1,0:T(8,128)}), f32[32,24,128]{2,1,0:T(8,128)S(1)}, u32[]{:S(2)}, u32[]{:S(2)}) async-start(f32[32,24,128]{2,1,0:T(8,128)} %route.1), calls=%async_computation.2 | async-start | bytes 786432 | tf_op jit(solution)/shard_map/all_to_all | solution.py:351
  23.9 7.7 %pack.1 = f32[32,128,128]{2,1,0:T(8,128)} custom-call(s32[1]{0:T(128)} %bitcast.self_ref.refs_0_, s32[32]{0:T(128)} %refs_1_.5, s32[32,128]{1,0:T(8,128)} %inner_ref.3, f32[128,4096]{1,0:T(8,128)} %slab_ref.3), custom_call_target="tpu_custom_call" | custom-call | tf_op jit(solution)/shard_map/pack/pallas_call | solution.py:405
  31.6 5.7 %all-to-all-done.2.refs_2_ = f32[32,24,128]{2,1,0:T(8,128)S(1)} async-done(((f32[32,24,128]{2,1,0:T(8,128)}), f32[32,24,128]{2,1,0:T(8,128)S(1)}, u32[]{:S(2)}, u32[]{:S(2)}) %all-to-all-start.2) | async-done | bytes 393248 | tf_op jit(solution)/shard_map/all_to_all | solution.py:351
  37.4 2.7 %all-to-all-start = ((f32[32,128,128]{2,1,0:T(8,128)}), f32[32,128,128]{2,1,0:T(8,128)S(1)}, u32[]{:S(2)}, u32[]{:S(2)}) async-start(f32[32,128,128]{2,1,0:T(8,128)} %pack.1), calls=%async_computation | async-start | bytes 4194304 | tf_op jit(solution)/shard_map/all_to_all | solution.py:351
  40.1 25.8 %factor.1 = (f32[128,384]{1,0:T(8,128)}, f32[32,128]{1,0:T(8,128)}, f32[32,128]{1,0:T(8,128)}) custom-call(s32[1]{0:T(128)} %bitcast.self_ref.refs_0_, s32[16]{0:T(128)} %lengths_ref.3, f32[32,24,128]{2,1,0:T(8,128)} %copy-done.1), custom_call_target="tpu_custom_call" | custom-call | tf_op jit(solution)/shard_map/factor/pallas_call | solution.py:425
  65.9 1.6 %collective-permute-start = (f32[1,32,128]{2,1,0:T(8,128)}, f32[1,32,128]{2,1,0:T(8,128)S(1)}, u32[]{:S(2)}, u32[]{:S(2)}) collective-permute-start(f32[1,32,128]{2,1,0:T(8,128)} %bitcast.7), channel_id=1, source_target_pairs={{0,16},{1,17},{2,18},{3,19},{4,20},{5,21},{6,22},{7,23},{8,24},{9,... | collective-permute-start | bytes 49160 | tf_op jit(solution)/shard_map/ppermute | solution.py:357
  68.3 1.6 %collective-permute-done = f32[1,32,128]{2,1,0:T(8,128)S(1)} collective-permute-done((f32[1,32,128]{2,1,0:T(8,128)}, f32[1,32,128]{2,1,0:T(8,128)S(1)}, u32[]{:S(2)}, u32[]{:S(2)}) %collective-permute-start) | collective-permute-done | bytes 16416 | tf_op jit(solution)/shard_map/ppermute | solution.py:357
  70.6 1.8 %collective-permute-start.1 = (f32[2,32,128]{2,1,0:T(8,128)S(1)}, f32[2,32,128]{2,1,0:T(8,128)S(1)}, u32[]{:S(2)}, u32[]{:S(2)}) collective-permute-start(f32[2,32,128]{2,1,0:T(8,128)S(1)} %pad_maximum_fusion.1), channel_id=1, source_target_pairs={{0,1},{1,0},{2,3},{3,2},{4,5},{5,4},{6,7},{7,6},{8,9},{9,8},{10,11... | collective-permute-start | bytes 98312 | tf_op jit(solution)/shard_map/ppermute | solution.py:357
  72.4 2.1 %collective-permute-done.1 = f32[2,32,128]{2,1,0:T(8,128)S(1)} collective-permute-done((f32[2,32,128]{2,1,0:T(8,128)S(1)}, f32[2,32,128]{2,1,0:T(8,128)S(1)}, u32[]{:S(2)}, u32[]{:S(2)}) %collective-permute-start.1) | collective-permute-done | bytes 32800 | tf_op jit(solution)/shard_map/ppermute | solution.py:357
  75.2 4.1 %collective-permute-start.4 = (f32[4,32,128]{2,1,0:T(8,128)S(1)}, f32[4,32,128]{2,1,0:T(8,128)S(1)}, u32[]{:S(2)}, u32[]{:S(2)}) collective-permute-start(f32[4,32,128]{2,1,0:T(8,128)S(1)} %pad_maximum_fusion), channel_id=1, source_target_pairs={{0,6},{1,7},{2,4},{3,5},{4,2},{5,3},{6,0},{7,1},{8,14},{9,15},{10,... | collective-permute-start | bytes 196616 | tf_op jit(solution)/shard_map/ppermute | solution.py:357
  79.3 3.2 %collective-permute-start.3 = (f32[4,32,128]{2,1,0:T(8,128)S(1)}, f32[4,32,128]{2,1,0:T(8,128)S(1)}, u32[]{:S(2)}, u32[]{:S(2)}) collective-permute-start(f32[4,32,128]{2,1,0:T(8,128)S(1)} %pad_maximum_fusion), channel_id=1, source_target_pairs={{0,4},{1,5},{2,6},{3,7},{4,0},{5,1},{6,2},{7,3},{8,12},{9,13},{10,... | collective-permute-start | bytes 196616 | tf_op jit(solution)/shard_map/ppermute | solution.py:357
  83.0 4.0 %collective-permute-done.2 = f32[4,32,128]{2,1,0:T(8,128)S(1)} collective-permute-done((f32[4,32,128]{2,1,0:T(8,128)S(1)}, f32[4,32,128]{2,1,0:T(8,128)S(1)}, u32[]{:S(2)}, u32[]{:S(2)}) %collective-permute-start.2) | collective-permute-done | bytes 65568 | tf_op jit(solution)/shard_map/ppermute | solution.py:357
  87.1 7.3 %collective-permute-done.3 = f32[4,32,128]{2,1,0:T(8,128)S(1)} collective-permute-done((f32[4,32,128]{2,1,0:T(8,128)S(1)}, f32[4,32,128]{2,1,0:T(8,128)S(1)}, u32[]{:S(2)}, u32[]{:S(2)}) %collective-permute-start.3) | collective-permute-done | bytes 65568 | tf_op jit(solution)/shard_map/ppermute | solution.py:357
  94.5 1.5 %collective-permute-done.5.refs_5_ = f32[16,32,128]{2,1,0:T(8,128)S(1)} collective-permute-done((f32[16,32,128]{2,1,0:T(8,128)S(1)}, f32[16,32,128]{2,1,0:T(8,128)S(1)}, u32[]{:S(2)}, u32[]{:S(2)}) %collective-permute-start.5) | collective-permute-done | bytes 262176 | tf_op jit(solution)/shard_map/ppermute | solution.py:357
  97.5 3.4 %residual.1.rest_2_ = f32[32,128]{1,0:T(8,128)} custom-call(s32[1]{0:T(128)} %bitcast.self_ref.refs_0_, s32[32]{0:T(128)} %refs_1_.5, f32[32,128,128]{2,1,0:T(8,128)} %copy-done, f32[32,128]{1,0:T(8,128)} %get-tuple-element.7.refs_3_, f32[16,32,128]{2,1,0:T(8,128)} %copy-done.2, f32[16,32,128]{2,1,0:T(8,128)} %copy-done.3), custom_call_target="tpu_custom_call" | custom-call | tf_op jit(solution)/shard_map/residual/pallas_call | solution.py:446
  100.8 2.0 %collective-permute-start.9 = (f32[32,128]{1,0:T(8,128)}, f32[32,128]{1,0:T(8,128)S(1)}, u32[]{:S(2)}, u32[]{:S(2)}) collective-permute-start(f32[32,128]{1,0:T(8,128)} %residual.1.rest_2_), channel_id=1, source_target_pairs={{0,30},{1,31},{2,0},{3,1},{4,2},{5,3},{6,4},{7,5},{8,6},{9,7},{10,... | collective-permute-start | bytes 49160 | tf_op jit(solution)/shard_map/ppermute | solution.py:346
  102.8 1.0 collective-permute-start.8
  103.8 1.1 collective-permute-start.7
  105.8 3.2 %arrange.1 = f32[4096,128]{1,0:T(8,128)} custom-call(s32[32]{0:T(128)} %refs_1_.5, f32[32,128,128]{2,1,0:T(8,128)} %copy-done), custom_call_target="tpu_custom_call" | custom-call | tf_op jit(solution)/shard_map/arrange/pallas_call | solution.py:439
  109.0 1.7 %collective-permute-done.7.rest_1_ = f32[32,128]{1,0:T(8,128)S(1)} collective-permute-done((f32[32,128]{1,0:T(8,128)}, f32[32,128]{1,0:T(8,128)S(1)}, u32[]{:S(2)}, u32[]{:S(2)}) %collective-permute-start.7) | collective-permute-done | bytes 16416 | tf_op jit(solution)/shard_map/ppermute | solution.py:346
  111.5 2.1 %finish.1 = f32[32,128]{1,0:T(8,128)} custom-call(s32[1]{0:T(128)} %bitcast.self_ref.refs_0_, s32[16]{0:T(128)} %lengths_ref.3, f32[128,384]{1,0:T(8,128)} %get-tuple-element.5.v_ref, f32[32,128]{1,0:T(8,128)} %get-tuple-element.6.z_ref, f32[32,128]{1,0:T(8,128)} %copy-done.7, f32[32,128]{1,0:T(8,128)} %copy-done.6, f32[32,128]{1,0:T(8,128)} %residual.1.rest_2_, ...), custom_call_target="tpu_custom_call" | custom-call | tf_op jit(solution)/shard_map/finish/pallas_call | solution.py:457
  (32 shorter events, 6.0 us)
Async XLA Ops:
  21.3 16.0 %all-to-all-start.2 = ((f32[32,24,128]{2,1,0:T(8,128)}), f32[32,24,128]{2,1,0:T(8,128)S(1)}, u32[]{:S(2)}, u32[]{:S(2)}) async-start(f32[32,24,128]{2,1,0:T(8,128)} %route.1), calls=%async_computation.2 | async-start | bytes 786432 | tf_op jit(solution)/shard_map/all_to_all | solution.py:351
  37.4 2.7 %copy-start.1 = (f32[32,24,128]{2,1,0:T(8,128)}, f32[32,24,128]{2,1,0:T(8,128)S(1)}, u32[]{:S(2)}) copy-start(f32[32,24,128]{2,1,0:T(8,128)S(1)} %all-to-all-done.2.refs_2_) | copy-start | bytes 1179652
  37.4 58.7 %all-to-all-start = ((f32[32,128,128]{2,1,0:T(8,128)}), f32[32,128,128]{2,1,0:T(8,128)S(1)}, u32[]{:S(2)}, u32[]{:S(2)}) async-start(f32[32,128,128]{2,1,0:T(8,128)} %pack.1), calls=%async_computation | async-start | bytes 4194304 | tf_op jit(solution)/shard_map/all_to_all | solution.py:351
  65.9 3.9 %collective-permute-start = (f32[1,32,128]{2,1,0:T(8,128)}, f32[1,32,128]{2,1,0:T(8,128)S(1)}, u32[]{:S(2)}, u32[]{:S(2)}) collective-permute-start(f32[1,32,128]{2,1,0:T(8,128)} %bitcast.7), channel_id=1, source_target_pairs={{0,16},{1,17},{2,18},{3,19},{4,20},{5,21},{6,22},{7,23},{8,24},{9,... | collective-permute-start | bytes 49160 | tf_op jit(solution)/shard_map/ppermute | solution.py:357
  70.6 3.9 %collective-permute-start.1 = (f32[2,32,128]{2,1,0:T(8,128)S(1)}, f32[2,32,128]{2,1,0:T(8,128)S(1)}, u32[]{:S(2)}, u32[]{:S(2)}) collective-permute-start(f32[2,32,128]{2,1,0:T(8,128)S(1)} %pad_maximum_fusion.1), channel_id=1, source_target_pairs={{0,1},{1,0},{2,3},{3,2},{4,5},{5,4},{6,7},{7,6},{8,9},{9,8},{10,11... | collective-permute-start | bytes 98312 | tf_op jit(solution)/shard_map/ppermute | solution.py:357
  75.2 19.2 %collective-permute-start.4 = (f32[4,32,128]{2,1,0:T(8,128)S(1)}, f32[4,32,128]{2,1,0:T(8,128)S(1)}, u32[]{:S(2)}, u32[]{:S(2)}) collective-permute-start(f32[4,32,128]{2,1,0:T(8,128)S(1)} %pad_maximum_fusion), channel_id=1, source_target_pairs={{0,6},{1,7},{2,4},{3,5},{4,2},{5,3},{6,0},{7,1},{8,14},{9,15},{10,... | collective-permute-start | bytes 196616 | tf_op jit(solution)/shard_map/ppermute | solution.py:357
  79.3 15.1 %collective-permute-start.3 = (f32[4,32,128]{2,1,0:T(8,128)S(1)}, f32[4,32,128]{2,1,0:T(8,128)S(1)}, u32[]{:S(2)}, u32[]{:S(2)}) collective-permute-start(f32[4,32,128]{2,1,0:T(8,128)S(1)} %pad_maximum_fusion), channel_id=1, source_target_pairs={{0,4},{1,5},{2,6},{3,7},{4,0},{5,1},{6,2},{7,3},{8,12},{9,13},{10,... | collective-permute-start | bytes 196616 | tf_op jit(solution)/shard_map/ppermute | solution.py:357
  82.5 4.6 %collective-permute-start.2 = (f32[4,32,128]{2,1,0:T(8,128)S(1)}, f32[4,32,128]{2,1,0:T(8,128)S(1)}, u32[]{:S(2)}, u32[]{:S(2)}) collective-permute-start(f32[4,32,128]{2,1,0:T(8,128)S(1)} %pad_maximum_fusion), channel_id=1, source_target_pairs={{0,2},{1,3},{2,0},{3,1},{4,6},{5,7},{6,4},{7,5},{8,10},{9,11},{10,... | collective-permute-start | bytes 196616 | tf_op jit(solution)/shard_map/ppermute | solution.py:357
  94.4 1.6 %copy-start.2 = (f32[16,32,128]{2,1,0:T(8,128)}, f32[16,32,128]{2,1,0:T(8,128)S(1)}, u32[]{:S(2)}) copy-start(f32[16,32,128]{2,1,0:T(8,128)S(1)} %constant_dynamic-update-slice_fusion.refs_4_) | copy-start | bytes 786436
  94.4 1.6 %collective-permute-start.5 = (f32[16,32,128]{2,1,0:T(8,128)S(1)}, f32[16,32,128]{2,1,0:T(8,128)S(1)}, u32[]{:S(2)}, u32[]{:S(2)}) collective-permute-start(f32[16,32,128]{2,1,0:T(8,128)S(1)} %constant_dynamic-update-slice_fusion.refs_4_), channel_id=1, source_target_pairs={{0,8},{1,9},{2,10},{3,11},{4,12},{5,13},{6,14},{7,15},{8,0},{9,1},... | collective-permute-start | bytes 786440 | tf_op jit(solution)/shard_map/ppermute | solution.py:357
  96.0 0.7 copy-start.3
  96.0 1.4 %copy-start = (f32[32,128,128]{2,1,0:T(8,128)}, f32[32,128,128]{2,1,0:T(8,128)S(1)}, u32[]{:S(2)}) copy-start(f32[32,128,128]{2,1,0:T(8,128)S(1)} %all-to-all-done.got_ref.refs_2_) | copy-start | bytes 6291460
  100.8 8.2 %collective-permute-start.9 = (f32[32,128]{1,0:T(8,128)}, f32[32,128]{1,0:T(8,128)S(1)}, u32[]{:S(2)}, u32[]{:S(2)}) collective-permute-start(f32[32,128]{1,0:T(8,128)} %residual.1.rest_2_), channel_id=1, source_target_pairs={{0,30},{1,31},{2,0},{3,1},{4,2},{5,3},{6,4},{7,5},{8,6},{9,7},{10,... | collective-permute-start | bytes 49160 | tf_op jit(solution)/shard_map/ppermute | solution.py:346
  102.8 6.2 %collective-permute-start.8 = (f32[32,128]{1,0:T(8,128)}, f32[32,128]{1,0:T(8,128)S(1)}, u32[]{:S(2)}, u32[]{:S(2)}) collective-permute-start(f32[32,128]{1,0:T(8,128)} %residual.1.rest_2_), channel_id=1, source_target_pairs={{0,31},{1,0},{2,1},{3,2},{4,3},{5,4},{6,5},{7,6},{8,7},{9,8},{10,9... | collective-permute-start | bytes 49160 | tf_op jit(solution)/shard_map/ppermute | solution.py:346
  103.8 7.0 %collective-permute-start.7 = (f32[32,128]{1,0:T(8,128)}, f32[32,128]{1,0:T(8,128)S(1)}, u32[]{:S(2)}, u32[]{:S(2)}) collective-permute-start(f32[32,128]{1,0:T(8,128)} %residual.1.rest_2_), channel_id=1, source_target_pairs={{0,1},{1,2},{2,3},{3,4},{4,5},{5,6},{6,7},{7,8},{8,9},{9,10},{10,1... | collective-permute-start | bytes 49160 | tf_op jit(solution)/shard_map/ppermute | solution.py:346
  104.9 6.1 %collective-permute-start.6 = (f32[32,128]{1,0:T(8,128)}, f32[32,128]{1,0:T(8,128)S(1)}, u32[]{:S(2)}, u32[]{:S(2)}) collective-permute-start(f32[32,128]{1,0:T(8,128)} %residual.1.rest_2_), channel_id=1, source_target_pairs={{0,2},{1,3},{2,4},{3,5},{4,6},{5,7},{6,8},{7,9},{8,10},{9,11},{10,... | collective-permute-start | bytes 49160 | tf_op jit(solution)/shard_map/ppermute | solution.py:346
  109.0 1.9 %copy-start.4 = (f32[32,128]{1,0:T(8,128)}, f32[32,128]{1,0:T(8,128)S(1)}, u32[]{:S(2)}) copy-start(f32[32,128]{1,0:T(8,128)S(1)} %collective-permute-done.9.rest_4_) | copy-start | bytes 49156
  109.0 1.9 %copy-start.5 = (f32[32,128]{1,0:T(8,128)}, f32[32,128]{1,0:T(8,128)S(1)}, u32[]{:S(2)}) copy-start(f32[32,128]{1,0:T(8,128)S(1)} %collective-permute-done.8.rest_3_) | copy-start | bytes 49156
  110.8 0.6 copy-start.6
  110.9 0.6 copy-start.7

commit v3 on v2

--- a/solution.py
+++ b/solution.py
@@ -1,3 +1,5 @@
+import math
+
 import jax
 import jax.numpy as jnp
 from jax import lax
@@ -30,7 +32,7 @@
     def step(t, found):
         return jnp.where(order_ref[t] == old_tile, t, found)
 
-    return lax.fori_loop(0, tiles, step, jnp.int32(0))
+    return lax.fori_loop(0, tiles, step, jnp.int32(0), unroll=8)
 
 
 def block_of(lengths_ref, place):
@@ -42,7 +44,9 @@
         return start + lengths_ref[e], first, length
 
     zero = jnp.int32(0)
-    _, first, length = lax.fori_loop(0, lengths_ref.shape[0], step, (zero, zero, zero + 1))
+    _, first, length = lax.fori_loop(
+        0, lengths_ref.shape[0], step, (zero, zero, zero + 1), unroll=8
+    )
     return first, length
 
 
@@ -161,7 +165,7 @@
                 send_ref[d, at : at + per_piece, :] = got_ref[source, SUB : SUB + per_piece, :]
         return 0
 
-    lax.fori_loop(0, tiles, fill, 0)
+    lax.fori_loop(0, tiles, fill, 0, unroll=4)
 
 
 def sweep(s):
@@ -296,15 +300,19 @@
     z_ref[...] = apply_rows(v_ref, b)
 
 
-def arrange_body(order_ref, got_ref, slab_ref):
+def arrange_body(order_ref, got_ref, slab_ref, sems):
     tiles = order_ref.shape[0]
     tile = got_ref.shape[1]
-
-    def move(t, _):
-        slab_ref[pl.ds(pl.multiple_of(t * tile, tile), tile), :] = got_ref[order_ref[t]]
-        return 0
-
-    lax.fori_loop(0, tiles, move, 0)
+    copies = [
+        pltpu.make_async_copy(
+            got_ref.at[order_ref[t]], slab_ref.at[t * tile : (t + 1) * tile, :], sems.at[t]
+        )
+        for t in range(tiles)
+    ]
+    for copy in copies:
+        copy.start()
+    for copy in copies:
+        copy.wait()
 
 
 def residual_body(self_ref, order_ref, got_ref, b_ref, *rest, flips):
@@ -343,13 +351,18 @@
 
 def shift(value, steps):
     count = lax.axis_size(AXES)
-    return lax.ppermute(value, AXES, [(s, (s + steps) % count) for s in range(count)])
+    pairs = [(s, (s + steps) % count) for s in range(count)]
+    return lax.ppermute(value, AXES, pairs)
 
 
 def exchange(value, rows):
     lanes = value.shape[-1]
     moved = lax.all_to_all(value.reshape(-1, lanes), AXES, 0, 0, tiled=True)
     return moved.reshape(-1, rows, lanes)
+
+
+def small_enough(dims):
+    return math.prod(dims) <= 1 << 19
 
 
 def swap(value, bit):
@@ -392,10 +405,20 @@
     hbm = pl.BlockSpec(memory_space=pl.ANY)
     shape = lambda *dims: jax.ShapeDtypeStruct(dims, f32)
 
+    def held(*dims):
+        return pltpu.VMEM(dims, f32) if small_enough(dims) else shape(*dims)
+
+    def hold(x):
+        return pltpu.with_memory_space_constraint(x, pltpu.VMEM) if small_enough(x.shape) else x
+
+
+    slab_bytes = 4 * normal_matrix.size
+    room = lambda slabs: pltpu.CompilerParams(vmem_limit_bytes=int(slabs * slab_bytes) + (4 << 20))
+
     small_rows = SUB if fit else 2 * SUB
     small = pl.pallas_call(
         near_body,
-        out_shape=shape(tiles * small_rows, tile),
+        out_shape=held(tiles * small_rows, tile),
         in_specs=[smem, smem, smem, vmem, vmem, hbm],
         out_specs=vmem,
         scratch_shapes=[pltpu.VMEM((2, tile, tile), f32), pltpu.SemaphoreType.DMA((2,))],
@@ -413,18 +436,18 @@
     routed_rows = MOSTT * SUB + (0 if fit else -(-MOSTT * per_piece // SUB) * SUB)
     routed = pl.pallas_call(
         lambda *refs: route_body(*refs, per_piece=per_piece),
-        out_shape=shape(tiles, routed_rows, tile),
+        out_shape=held(tiles, routed_rows, tile),
         in_specs=[smem, smem, vmem],
         out_specs=vmem,
         scratch_shapes=[pltpu.SMEM((tiles,), jnp.int32)],
         name="route",
-    )(tile_order, block_lengths, small_got)
+    )(tile_order, block_lengths, hold(small_got))
     block_parts = exchange(routed, routed_rows)
     tiles_got = exchange(tiles_out, tile)
 
     inverse_rows, own_sides, z = pl.pallas_call(
         lambda *refs: factor_body(*refs, per_piece=per_piece),
-        out_shape=(shape(tile, MOSTT * tile), shape(rhs, tile), shape(rhs, tile)),
+        out_shape=(held(tile, MOSTT * tile), held(rhs, tile), held(rhs, tile)),
         in_specs=[smem, smem, vmem],
         out_specs=(vmem, vmem, vmem),
         scratch_shapes=[
@@ -433,24 +456,28 @@
             pltpu.VMEM((MOSTT, rhs, tile), f32),
         ],
         name="factor",
-    )(me, block_lengths, block_parts)
+        compiler_params=room(1),
+    )(me, block_lengths, hold(block_parts))
 
     iterate, flips = spread(z)
     slab = pl.pallas_call(
         arrange_body,
         out_shape=shape(tiles * tile, tile),
         in_specs=[smem, vmem],
-        out_specs=vmem,
+        out_specs=hbm,
+        scratch_shapes=[pltpu.SemaphoreType.DMA((tiles,))],
         name="arrange",
-    )(tile_order, tiles_got)
+    compiler_params=room(1),
+    )(tile_order, hold(tiles_got))
     residual = pl.pallas_call(
         lambda *refs: residual_body(*refs, flips=flips),
-        out_shape=shape(rhs, tile),
+        out_shape=held(rhs, tile),
         in_specs=[smem, smem, vmem, vmem] + [vmem] * len(iterate),
         out_specs=vmem,
         scratch_shapes=[pltpu.VMEM((rhs, tiles * tile), f32)],
         name="residual",
-    )(me, tile_order, tiles_got, own_sides, *iterate)
+        compiler_params=room(3),
+    )(me, tile_order, hold(tiles_got), hold(own_sides), *map(hold, iterate))
     near = [
         residual if o == 0 else shift(residual, -o) for o in range(1 - MOSTT, MOSTT)
     ]
@@ -461,7 +488,8 @@
         out_specs=vmem,
         scratch_shapes=[pltpu.VMEM((len(near), rhs, tile), f32)],
         name="finish",
-    )(me, block_lengths, inverse_rows, z, *near)
+        compiler_params=room(0.5),
+    )(me, block_lengths, hold(inverse_rows), hold(z), *map(hold, near))
     return slab, solved.T
 
 

time: 114 us -> 108 us (0.947)
  waiting for transfers between devices: 24.2 us -> 32.6 us
  Pallas kernels: 47.5 us -> 41.3 us
  starting transfers between devices: 21.6 us -> 17.8 us
  local copies, waits for them, and re-layouts: 2.82 us -> 0.03 us
  other arithmetic: 1.44 us -> 0.01 us
    ppermute x6, waiting for transfers between devices: 16.5 us -> 23.7 us  [swap(): return lax.ppermute(value, AXES, [(s, s ^ bit) for s in range(count)])]
    ppermute x6, starting transfers between devices: 11.3 us -> 7.5 us  [swap(): return lax.ppermute(value, AXES, [(s, s ^ bit) for s in range(count)])]
    unnamed x21 -> x9, local copies, waits for them, and re-layouts: 2.81 us -> 0.03 us
    pallas_call x1, Pallas kernels: 3.35 us -> 1.64 us  [body(): pl.pallas_call(lambda *refs: residual_body(*refs, flips=flips), out_shape...]
    concatenate x2, other arithmetic: 1.44 us -> 0.01 us  [spread(): held = jnp.concatenate([held, swap(held, bit)], axis=0)]
    pallas_call x1, Pallas kernels: 25.8 us -> 24.6 us  [body(): pl.pallas_call(lambda *refs: factor_body(*refs, per_piece=per_piece), out...]
  transfers between devices with their start and end apart: 12 -> 12, of which waited for: 8 -> 8; matrix products, arithmetic and copies ran while one was open for 2% -> 0% of each run, Pallas kernels for 32% -> 32%
where the time goes in v3:
time: 108 us; the launch traced here: 107 us
  Pallas kernels  41.3 us (38%)
  waiting for transfers between devices  32.6 us (30%)
  starting transfers between devices  17.8 us (16%)
  blocking collectives  14.9 us (14%)
    pallas_call x1, Pallas kernels, body(): pl.pallas_call(lambda *refs: factor_body(*refs, per_piece=per_piece), out...  24.6 us
    ppermute x6, waiting for transfers between devices, swap(): return lax.ppermute(value, AXES, [(s, s ^ bit) for s in range(count)])  23.7 us
    all_to_all x1, blocking collectives, exchange(): moved = lax.all_to_all(value.reshape(-1, lanes), AXES, 0, 0, tiled=True)  14.9 us
    ppermute x6, starting transfers between devices, swap(): return lax.ppermute(value, AXES, [(s, s ^ bit) for s in range(count)])  7.5 us
    pallas_call x1, Pallas kernels, body(): pl.pallas_call(pack_body, out_shape=shape(tiles, tile, tile), in_specs=[s...  7.39 us
    all_to_all x2, waiting for transfers between devices, exchange(): moved = lax.all_to_all(value.reshape(-1, lanes), AXES, 0, 0, tiled=True)  6.03 us
    all_to_all x2, starting transfers between devices, exchange(): moved = lax.all_to_all(value.reshape(-1, lanes), AXES, 0, 0, tiled=True)  5.32 us
    ppermute x4, starting transfers between devices, shift(): return lax.ppermute(value, AXES, pairs)  5 us
  transfers between devices with their start and end apart: 12, of which 8 were waited for; matrix products, arithmetic and copies ran while one was open for 0% of the time, Pallas kernels for 32%

profile of v3, /device:TPU:0, one launch (start us, length us, event | category | flops | bytes accessed | tf_op | source)
XLA Modules:
  0.0 107.4 jit_solution(871412530093789840)
XLA Ops:
  0.6 2.2 %near.1 = f32[256,128]{1,0:T(8,128)S(1)} custom-call(s32[1]{0:T(128)} %bitcast.self_ref.refs_0_, s32[32]{0:T(128)} %refs_1_.5, s32[16]{0:T(128)} %lengths_ref.3, s32[32,128]{1,0:T(8,128)} %inner_ref.3, f32[32,128]{1,0:T(8,128)} %bitcast.10, f32[128,4096]{1,0:T(8,128)} %slab_ref.3), custom_call_target="tpu_custom_call" | custom-call | tf_op jit(solution)/shard_map/near/pallas_call | solution.py:419
  2.9 14.9 %all_to_all.21.refs_2_ = f32[32,8,128]{2,1,0:T(8,128)S(1)} all-to-all(f32[32,8,128]{2,1,0:T(8,128)S(1)} %bitcast.6), channel_id=1, replica_groups=mesh['gx'=4,'gy'=8] {'gx','gy'}, dimensions={0} | all-to-all | bytes 262144 | tf_op jit(solution)/shard_map/all_to_all | solution.py:360
  17.8 1.8 %route.1 = f32[32,24,128]{2,1,0:T(8,128)} custom-call(s32[32]{0:T(128)} %refs_1_.5, s32[16]{0:T(128)} %lengths_ref.3, f32[32,8,128]{2,1,0:T(8,128)S(1)} %all_to_all.21.refs_2_), custom_call_target="tpu_custom_call" | custom-call | tf_op jit(solution)/shard_map/route/pallas_call | solution.py:437
  19.6 2.6 %all-to-all-start.2 = ((f32[32,24,128]{2,1,0:T(8,128)}), f32[32,24,128]{2,1,0:T(8,128)S(1)}, u32[]{:S(2)}, u32[]{:S(2)}) async-start(f32[32,24,128]{2,1,0:T(8,128)} %route.1), calls=%async_computation.2 | async-start | bytes 786432 | tf_op jit(solution)/shard_map/all_to_all | solution.py:360
  22.2 7.4 %pack.1 = f32[32,128,128]{2,1,0:T(8,128)} custom-call(s32[1]{0:T(128)} %bitcast.self_ref.refs_0_, s32[32]{0:T(128)} %refs_1_.5, s32[32,128]{1,0:T(8,128)} %inner_ref.3, f32[128,4096]{1,0:T(8,128)} %slab_ref.3), custom_call_target="tpu_custom_call" | custom-call | tf_op jit(solution)/shard_map/pack/pallas_call | solution.py:428
  29.6 6.0 %all-to-all-done.2.refs_2_ = f32[32,24,128]{2,1,0:T(8,128)S(1)} async-done(((f32[32,24,128]{2,1,0:T(8,128)}), f32[32,24,128]{2,1,0:T(8,128)S(1)}, u32[]{:S(2)}, u32[]{:S(2)}) %all-to-all-start.2) | async-done | bytes 393248 | tf_op jit(solution)/shard_map/all_to_all | solution.py:360
  35.6 2.7 %all-to-all-start = ((f32[32,128,128]{2,1,0:T(8,128)}), f32[32,128,128]{2,1,0:T(8,128)S(1)}, u32[]{:S(2)}, u32[]{:S(2)}) async-start(f32[32,128,128]{2,1,0:T(8,128)} %pack.1), calls=%async_computation | async-start | bytes 4194304 | tf_op jit(solution)/shard_map/all_to_all | solution.py:360
  38.3 24.6 %factor.1 = (f32[128,384]{1,0:T(8,128)S(1)}, f32[32,128]{1,0:T(8,128)S(1)}, f32[32,128]{1,0:T(8,128)S(1)}) custom-call(s32[1]{0:T(128)} %bitcast.self_ref.refs_0_, s32[16]{0:T(128)S(1)} %copy-done.1, f32[32,24,128]{2,1,0:T(8,128)S(1)} %all-to-all-done.2.refs_2_), custom_call_target="tpu_custom_call" | custom-call | tf_op jit(solution)/shard_map/factor/pallas_call | solution.py:448
  63.0 1.7 %collective-permute-start = (f32[1,32,128]{2,1,0:T(8,128)S(1)}, f32[1,32,128]{2,1,0:T(8,128)S(1)}, u32[]{:S(2)}, u32[]{:S(2)}) collective-permute-start(f32[1,32,128]{2,1,0:T(8,128)S(1)} %bitcast.7), channel_id=1, source_target_pairs={{0,16},{1,17},{2,18},{3,19},{4,20},{5,21},{6,22},{7,23},{8,24},{9,... | collective-permute-start | bytes 49160 | tf_op jit(solution)/shard_map/ppermute | solution.py:370
  64.7 2.5 %collective-permute-done = f32[1,32,128]{2,1,0:T(8,128)S(1)} collective-permute-done((f32[1,32,128]{2,1,0:T(8,128)S(1)}, f32[1,32,128]{2,1,0:T(8,128)S(1)}, u32[]{:S(2)}, u32[]{:S(2)}) %collective-permute-start) | collective-permute-done | bytes 16416 | tf_op jit(solution)/shard_map/ppermute | solution.py:370
  67.2 1.3 %collective-permute-start.1 = (f32[2,32,128]{2,1,0:T(8,128)S(1)}, f32[2,32,128]{2,1,0:T(8,128)S(1)}, u32[]{:S(2)}, u32[]{:S(2)}) collective-permute-start(f32[2,32,128]{2,1,0:T(8,128)S(1)} %pad_maximum_fusion.1), channel_id=1, source_target_pairs={{0,1},{1,0},{2,3},{3,2},{4,5},{5,4},{6,7},{7,6},{8,9},{9,8},{10,11... | collective-permute-start | bytes 98312 | tf_op jit(solution)/shard_map/ppermute | solution.py:370
  68.4 2.6 %collective-permute-done.1 = f32[2,32,128]{2,1,0:T(8,128)S(1)} collective-permute-done((f32[2,32,128]{2,1,0:T(8,128)S(1)}, f32[2,32,128]{2,1,0:T(8,128)S(1)}, u32[]{:S(2)}, u32[]{:S(2)}) %collective-permute-start.1) | collective-permute-done | bytes 32800 | tf_op jit(solution)/shard_map/ppermute | solution.py:370
  71.1 3.6 %collective-permute-start.4 = (f32[4,32,128]{2,1,0:T(8,128)S(1)}, f32[4,32,128]{2,1,0:T(8,128)S(1)}, u32[]{:S(2)}, u32[]{:S(2)}) collective-permute-start(f32[4,32,128]{2,1,0:T(8,128)S(1)} %pad_maximum_fusion), channel_id=1, source_target_pairs={{0,6},{1,7},{2,4},{3,5},{4,2},{5,3},{6,0},{7,1},{8,14},{9,15},{10,... | collective-permute-start | bytes 196616 | tf_op jit(solution)/shard_map/ppermute | solution.py:370
  75.5 4.5 %collective-permute-done.2 = f32[4,32,128]{2,1,0:T(8,128)S(1)} collective-permute-done((f32[4,32,128]{2,1,0:T(8,128)S(1)}, f32[4,32,128]{2,1,0:T(8,128)S(1)}, u32[]{:S(2)}, u32[]{:S(2)}) %collective-permute-start.2) | collective-permute-done | bytes 65568 | tf_op jit(solution)/shard_map/ppermute | solution.py:370
  80.0 12.6 %collective-permute-done.3 = f32[4,32,128]{2,1,0:T(8,128)S(1)} collective-permute-done((f32[4,32,128]{2,1,0:T(8,128)S(1)}, f32[4,32,128]{2,1,0:T(8,128)S(1)}, u32[]{:S(2)}, u32[]{:S(2)}) %collective-permute-start.3) | collective-permute-done | bytes 65568 | tf_op jit(solution)/shard_map/ppermute | solution.py:370
  92.7 1.5 %collective-permute-done.5.refs_5_ = f32[16,32,128]{2,1,0:T(8,128)S(1)} collective-permute-done((f32[16,32,128]{2,1,0:T(8,128)S(1)}, f32[16,32,128]{2,1,0:T(8,128)S(1)}, u32[]{:S(2)}, u32[]{:S(2)}) %collective-permute-start.5) | collective-permute-done | bytes 262176 | tf_op jit(solution)/shard_map/ppermute | solution.py:370
  94.2 1.6 %residual.1.rest_2_ = f32[32,128]{1,0:T(8,128)S(1)} custom-call(s32[1]{0:T(128)} %bitcast.self_ref.refs_0_, s32[32]{0:T(128)S(1)} %copy-done, f32[32,128,128]{2,1,0:T(8,128)S(1)} %all-to-all-done.got_ref.refs_2_, f32[32,128]{1,0:T(8,128)S(1)} %get-tuple-element.7.refs_3_, f32[16,32,128]{2,1,0:T(8,128)S(1)} %constant_dynamic-update-slice_fusion.refs_4_, ...), custom_call_target="tpu_custom_call" | custom-call | tf_op jit(solution)/shard_map/residual/pallas_call | solution.py:472
  95.9 2.1 %collective-permute-start.9 = (f32[32,128]{1,0:T(8,128)S(1)}, f32[32,128]{1,0:T(8,128)S(1)}, u32[]{:S(2)}, u32[]{:S(2)}) collective-permute-start(f32[32,128]{1,0:T(8,128)S(1)} %residual.1.rest_2_), channel_id=1, source_target_pairs={{0,30},{1,31},{2,0},{3,1},{4,2},{5,3},{6,4},{7,5},{8,6},{9,7},{10,... | collective-permute-start | bytes 49160 | tf_op jit(solution)/shard_map/ppermute | solution.py:355
  98.0 1.0 collective-permute-start.8
  98.9 1.1 collective-permute-start.7
  100.0 0.9 collective-permute-start.6
  100.9 2.1 %arrange.1 = f32[4096,128]{1,0:T(8,128)} custom-call(s32[32]{0:T(128)S(1)} %copy-done, f32[32,128,128]{2,1,0:T(8,128)S(1)} %all-to-all-done.got_ref.refs_2_), custom_call_target="tpu_custom_call" | custom-call | tf_op jit(solution)/shard_map/arrange/pallas_call | solution.py:463
  103.0 2.7 %collective-permute-done.7.rest_1_ = f32[32,128]{1,0:T(8,128)S(1)} collective-permute-done((f32[32,128]{1,0:T(8,128)S(1)}, f32[32,128]{1,0:T(8,128)S(1)}, u32[]{:S(2)}, u32[]{:S(2)}) %collective-permute-start.7) | collective-permute-done | bytes 16416 | tf_op jit(solution)/shard_map/ppermute | solution.py:355
  105.9 1.5 %finish.1 = f32[32,128]{1,0:T(8,128)} custom-call(s32[1]{0:T(128)} %bitcast.self_ref.refs_0_, s32[16]{0:T(128)S(1)} %copy-done.1, f32[128,384]{1,0:T(8,128)S(1)} %get-tuple-element.5.v_ref, f32[32,128]{1,0:T(8,128)S(1)} %get-tuple-element.6.z_ref, f32[32,128]{1,0:T(8,128)S(1)} %collective-permute-done.6.rest_0_, ...), custom_call_target="tpu_custom_call" | custom-call | tf_op jit(solution)/shard_map/finish/pallas_call | solution.py:484
  (20 shorter events, 1.2 us)
Async XLA Ops:
  19.6 16.0 %all-to-all-start.2 = ((f32[32,24,128]{2,1,0:T(8,128)}), f32[32,24,128]{2,1,0:T(8,128)S(1)}, u32[]{:S(2)}, u32[]{:S(2)}) async-start(f32[32,24,128]{2,1,0:T(8,128)} %route.1), calls=%async_computation.2 | async-start | bytes 786432 | tf_op jit(solution)/shard_map/all_to_all | solution.py:360
  29.6 8.8 %copy-start.1 = (s32[16]{0:T(128)S(1)}, s32[16]{0:T(128)}, u32[]{:S(2)}) copy-start(s32[16]{0:T(128)} %lengths_ref.3) | copy-start | bytes 196
  29.6 64.7 %copy-start = (s32[32]{0:T(128)S(1)}, s32[32]{0:T(128)}, u32[]{:S(2)}) copy-start(s32[32]{0:T(128)} %refs_1_.5) | copy-start | bytes 388
  35.6 58.6 %all-to-all-start = ((f32[32,128,128]{2,1,0:T(8,128)}), f32[32,128,128]{2,1,0:T(8,128)S(1)}, u32[]{:S(2)}, u32[]{:S(2)}) async-start(f32[32,128,128]{2,1,0:T(8,128)} %pack.1), calls=%async_computation | async-start | bytes 4194304 | tf_op jit(solution)/shard_map/all_to_all | solution.py:360
  63.0 4.2 %collective-permute-start = (f32[1,32,128]{2,1,0:T(8,128)S(1)}, f32[1,32,128]{2,1,0:T(8,128)S(1)}, u32[]{:S(2)}, u32[]{:S(2)}) collective-permute-start(f32[1,32,128]{2,1,0:T(8,128)S(1)} %bitcast.7), channel_id=1, source_target_pairs={{0,16},{1,17},{2,18},{3,19},{4,20},{5,21},{6,22},{7,23},{8,24},{9,... | collective-permute-start | bytes 49160 | tf_op jit(solution)/shard_map/ppermute | solution.py:370
  67.2 3.9 %collective-permute-start.1 = (f32[2,32,128]{2,1,0:T(8,128)S(1)}, f32[2,32,128]{2,1,0:T(8,128)S(1)}, u32[]{:S(2)}, u32[]{:S(2)}) collective-permute-start(f32[2,32,128]{2,1,0:T(8,128)S(1)} %pad_maximum_fusion.1), channel_id=1, source_target_pairs={{0,1},{1,0},{2,3},{3,2},{4,5},{5,4},{6,7},{7,6},{8,9},{9,8},{10,11... | collective-permute-start | bytes 98312 | tf_op jit(solution)/shard_map/ppermute | solution.py:370
  71.1 21.5 %collective-permute-start.4 = (f32[4,32,128]{2,1,0:T(8,128)S(1)}, f32[4,32,128]{2,1,0:T(8,128)S(1)}, u32[]{:S(2)}, u32[]{:S(2)}) collective-permute-start(f32[4,32,128]{2,1,0:T(8,128)S(1)} %pad_maximum_fusion), channel_id=1, source_target_pairs={{0,6},{1,7},{2,4},{3,5},{4,2},{5,3},{6,0},{7,1},{8,14},{9,15},{10,... | collective-permute-start | bytes 196616 | tf_op jit(solution)/shard_map/ppermute | solution.py:370
  74.7 17.9 %collective-permute-start.3 = (f32[4,32,128]{2,1,0:T(8,128)S(1)}, f32[4,32,128]{2,1,0:T(8,128)S(1)}, u32[]{:S(2)}, u32[]{:S(2)}) collective-permute-start(f32[4,32,128]{2,1,0:T(8,128)S(1)} %pad_maximum_fusion), channel_id=1, source_target_pairs={{0,4},{1,5},{2,6},{3,7},{4,0},{5,1},{6,2},{7,3},{8,12},{9,13},{10,... | collective-permute-start | bytes 196616 | tf_op jit(solution)/shard_map/ppermute | solution.py:370
  75.5 4.5 %collective-permute-start.2 = (f32[4,32,128]{2,1,0:T(8,128)S(1)}, f32[4,32,128]{2,1,0:T(8,128)S(1)}, u32[]{:S(2)}, u32[]{:S(2)}) collective-permute-start(f32[4,32,128]{2,1,0:T(8,128)S(1)} %pad_maximum_fusion), channel_id=1, source_target_pairs={{0,2},{1,3},{2,0},{3,1},{4,6},{5,7},{6,4},{7,5},{8,10},{9,11},{10,... | collective-permute-start | bytes 196616 | tf_op jit(solution)/shard_map/ppermute | solution.py:370
  92.6 1.6 %collective-permute-start.5 = (f32[16,32,128]{2,1,0:T(8,128)S(1)}, f32[16,32,128]{2,1,0:T(8,128)S(1)}, u32[]{:S(2)}, u32[]{:S(2)}) collective-permute-start(f32[16,32,128]{2,1,0:T(8,128)S(1)} %constant_dynamic-update-slice_fusion.refs_4_), channel_id=1, source_target_pairs={{0,8},{1,9},{2,10},{3,11},{4,12},{5,13},{6,14},{7,15},{8,0},{9,1},... | collective-permute-start | bytes 786440 | tf_op jit(solution)/shard_map/ppermute | solution.py:370
  95.9 7.1 %collective-permute-start.9 = (f32[32,128]{1,0:T(8,128)S(1)}, f32[32,128]{1,0:T(8,128)S(1)}, u32[]{:S(2)}, u32[]{:S(2)}) collective-permute-start(f32[32,128]{1,0:T(8,128)S(1)} %residual.1.rest_2_), channel_id=1, source_target_pairs={{0,30},{1,31},{2,0},{3,1},{4,2},{5,3},{6,4},{7,5},{8,6},{9,7},{10,... | collective-permute-start | bytes 49160 | tf_op jit(solution)/shard_map/ppermute | solution.py:355
  98.0 5.0 %collective-permute-start.8 = (f32[32,128]{1,0:T(8,128)S(1)}, f32[32,128]{1,0:T(8,128)S(1)}, u32[]{:S(2)}, u32[]{:S(2)}) collective-permute-start(f32[32,128]{1,0:T(8,128)S(1)} %residual.1.rest_2_), channel_id=1, source_target_pairs={{0,31},{1,0},{2,1},{3,2},{4,3},{5,4},{6,5},{7,6},{8,7},{9,8},{10,9... | collective-permute-start | bytes 49160 | tf_op jit(solution)/shard_map/ppermute | solution.py:355
  98.9 6.8 %collective-permute-start.7 = (f32[32,128]{1,0:T(8,128)S(1)}, f32[32,128]{1,0:T(8,128)S(1)}, u32[]{:S(2)}, u32[]{:S(2)}) collective-permute-start(f32[32,128]{1,0:T(8,128)S(1)} %residual.1.rest_2_), channel_id=1, source_target_pairs={{0,1},{1,2},{2,3},{3,4},{4,5},{5,6},{6,7},{7,8},{8,9},{9,10},{10,1... | collective-permute-start | bytes 49160 | tf_op jit(solution)/shard_map/ppermute | solution.py:355
  100.0 5.9 %collective-permute-start.6 = (f32[32,128]{1,0:T(8,128)S(1)}, f32[32,128]{1,0:T(8,128)S(1)}, u32[]{:S(2)}, u32[]{:S(2)}) collective-permute-start(f32[32,128]{1,0:T(8,128)S(1)} %residual.1.rest_2_), channel_id=1, source_target_pairs={{0,2},{1,3},{2,4},{3,5},{4,6},{5,7},{6,8},{7,9},{8,10},{9,11},{10,... | collective-permute-start | bytes 49160 | tf_op jit(solution)/shard_map/ppermute | solution.py:355

commit v4 on v3

--- a/solution.py
+++ b/solution.py
@@ -67,52 +67,47 @@
     return 4 * rhs == tile
 
 
-def near_body(self_ref, order_ref, lengths_ref, inner_ref, sides_ref, slab_ref, small_ref, near_ref, sems):
+def near_body(self_ref, order_ref, lengths_ref, sides_ref, slab_ref, small_ref, near_ref, sems):
     tile = slab_ref.shape[0]
     tiles = order_ref.shape[0]
     rhs = sides_ref.shape[0]
     me = self_ref[0]
+    pieces = 2 * tile // SUB
+    rows = small_ref.shape[0] // tiles
+    half = tile // 2
+    fit = sides_fit(tile, rhs)
+
+    def fetch(i, old_tile):
+        at = pl.ds(pl.multiple_of(old_tile * tile, tile), tile)
+        target = small_ref.at[i * tile : (i + 1) * tile, :] if fit else near_ref.at[i]
+        copy = pltpu.make_async_copy(slab_ref.at[:, at], target, sems.at[i])
+        copy.start()
+        return copy
+
+    own = fetch(0, me)
     place = place_of_tile(order_ref, tiles, me)
     first, _ = block_of(lengths_ref, place)
     position = place - first
     after = jnp.where(position == MOSTT - 1, 0, position + 1)
-    beside = jnp.minimum(first + after, tiles - 1)
-    places = (place, beside)
-    copies = []
-    for i, t in enumerate(places):
-        at = pl.ds(pl.multiple_of(order_ref[t] * tile, tile), tile)
-        copies.append(pltpu.make_async_copy(slab_ref.at[:, at], near_ref.at[i], sems.at[i]))
-        copies[-1].start()
-    own_inner = inner_ref[pl.ds(place, 1), :]
-    row_hot = row_choice(own_inner, tile)
-    turned = jnp.take_along_axis(
-        sides_ref[...], jnp.broadcast_to(own_inner, (rhs, tile)), axis=1
-    )
-    pieces = 2 * tile // SUB
-    rows = small_ref.shape[0] // tiles
-    half = tile // 2
-    lane = lax.broadcasted_iota(jnp.int32, (SUB, tile), 1)
+    beside = fetch(1, order_ref[jnp.minimum(first + after, tiles - 1)])
     if small_ref.shape[0] > pieces * rows:
         small_ref[pieces * rows :, :] = jnp.zeros((small_ref.shape[0] - pieces * rows, tile), jnp.float32)
-    for i, t in enumerate(places):
-        copies[i].wait()
-        moved = split_rows(row_hot, near_ref[i])
-        chosen = jnp.broadcast_to(inner_ref[pl.ds(t, 1), :], (tile, tile))
-        moved = jnp.take_along_axis(moved, chosen, axis=1)
-        if i == 0 and sides_fit(tile, rhs):
-            extra = jnp.concatenate([turned, pltpu.roll(turned, half, 1)], axis=0)
-        for k in range(pieces // 2):
-            chunk = moved[k * SUB : (k + 1) * SUB, :]
-            if i == 0 and sides_fit(tile, rhs) and k * SUB >= half:
-                chunk = jnp.where(lane < half, extra[k * SUB - half : (k + 1) * SUB - half, :], chunk)
-            at = (i * (pieces // 2) + k) * rows
-            small_ref[at : at + SUB, :] = chunk
-    if not sides_fit(tile, rhs):
+    own.wait()
+    if fit:
+        sides = sides_ref[...]
+        lane = lax.broadcasted_iota(jnp.int32, (tile - half, tile), 1)
+        extra = jnp.concatenate([sides, pltpu.roll(sides, half, 1)], axis=0)
+        small_ref[half:tile, :] = jnp.where(lane < half, extra, small_ref[half:tile, :])
+        beside.wait()
+    else:
+        beside.wait()
         per_piece = rhs // pieces
         for k in range(pieces):
-            at = k * rows + SUB
-            small_ref[at : at + SUB, :] = jnp.zeros((SUB, tile), jnp.float32)
-            small_ref[at : at + per_piece, :] = turned[k * per_piece : (k + 1) * per_piece, :]
+            at = k * rows
+            start = k * SUB % tile
+            small_ref[at : at + SUB, :] = near_ref[k * SUB // tile, start : start + SUB, :]
+            small_ref[at + SUB : at + 2 * SUB, :] = jnp.zeros((SUB, tile), jnp.float32)
+            small_ref[at + SUB : at + SUB + per_piece, :] = sides_ref[k * per_piece : (k + 1) * per_piece, :]
 
 
 def pack_body(self_ref, order_ref, inner_ref, slab_ref, send_ref, rows_ref):
@@ -146,12 +141,10 @@
 
     def block(e, start):
         for j in range(MOSTT):
-            @pl.when(j < lengths_ref[e])
-            def _():
-                first_ref[start + j] = start
+            first_ref[start + j] = start
         return start + lengths_ref[e]
 
-    lax.fori_loop(0, lengths_ref.shape[0], block, jnp.int32(0))
+    lax.fori_loop(0, lengths_ref.shape[0], block, jnp.int32(0), unroll=8)
     spare = send_ref.shape[1] - MOSTT * SUB
 
     def fill(d, _):
@@ -250,7 +243,7 @@
     return chosen
 
 
-def factor_body(self_ref, lengths_ref, got_ref, v_ref, b_ref, z_ref, f_ref, o_ref, bs_ref, *, per_piece):
+def factor_body(self_ref, lengths_ref, inner_ref, got_ref, v_ref, b_ref, z_ref, f_ref, o_ref, bs_ref, *, per_piece):
     tile = got_ref.shape[2]
     rhs = b_ref.shape[0]
     pieces = 2 * tile // SUB
@@ -259,26 +252,35 @@
     position = self_ref[0] - first
     row = lax.broadcasted_iota(jnp.int32, (tile, tile), 0)
     lane = lax.broadcasted_iota(jnp.int32, (tile, tile), 1)
+    inner = [inner_ref[pl.ds(jnp.minimum(first + m, inner_ref.shape[0] - 1), 1), :] for m in range(MOSTT)]
+    hot = [row_choice(order, tile) for order in inner]
+
+    def ordered(x, m, n):
+        moved = split_rows(hot[m], x)
+        return jnp.take_along_axis(moved, jnp.broadcast_to(inner[n], (tile, tile)), axis=1)
+
     for m in range(MOSTT):
         pair_inside = m + 1 < length if m < MOSTT - 1 else m < length
         for k in range(pieces // 2):
             at = slice(k * SUB, (k + 1) * SUB)
             f_ref[m, at, :] = got_ref[k, m * SUB : (m + 1) * SUB, :]
-            beside = got_ref[k + pieces // 2, m * SUB : (m + 1) * SUB, :]
-            o_ref[m, at, :] = jnp.where(pair_inside, beside, 0.0)
+            o_ref[m, at, :] = got_ref[k + pieces // 2, m * SUB : (m + 1) * SUB, :]
+        o_ref[m] = jnp.where(pair_inside, ordered(o_ref[m], m, (m + 1) % MOSTT), 0.0)
         own = f_ref[m]
         if sides_fit(tile, rhs):
             low = own[half : half + rhs, :]
             high = pltpu.roll(own[half + rhs :, :], half, 1)
             side = jnp.where(lane[:rhs, :] < half, low, high)
             own = jnp.where((row >= half) & (lane < half), own.T, own)
-            bs_ref[m] = jnp.where(m < length, side, 0.0)
+            bs_ref[m] = side
         else:
             for k in range(pieces):
                 start = MOSTT * SUB + m * per_piece
                 part = got_ref[k, start : start + per_piece, :]
-                bs_ref[m, k * per_piece : (k + 1) * per_piece, :] = jnp.where(m < length, part, 0.0)
-        f_ref[m] = jnp.where(m < length, own, jnp.where(row == lane, 1.0, 0.0))
+                bs_ref[m, k * per_piece : (k + 1) * per_piece, :] = part
+        side = jnp.take_along_axis(bs_ref[m], jnp.broadcast_to(inner[m], (rhs, tile)), axis=1)
+        bs_ref[m] = jnp.where(m < length, side, 0.0)
+        f_ref[m] = jnp.where(m < length, ordered(own, m, m), jnp.where(row == lane, 1.0, 0.0))
     a01 = o_ref[0]
     a12 = o_ref[1]
     a20 = o_ref[2]
@@ -315,23 +317,17 @@
         copy.wait()
 
 
-def residual_body(self_ref, order_ref, got_ref, b_ref, *rest, flips):
-    part_refs, r_ref, x_ref = rest[:-2], rest[-2], rest[-1]
-    _, tile = b_ref.shape
-    tiles = order_ref.shape[0]
+def residual_body(self_ref, order_ref, got_ref, b_ref, part_ref, r_ref, x_ref, tiles_ref, *, flips):
+    tile = b_ref.shape[1]
     me = self_ref[0]
-    j = 0
-    for part_ref in part_refs:
-        for i in range(part_ref.shape[0]):
-            at = pl.multiple_of(order_ref[me ^ flips[j]] * tile, tile)
-            x_ref[:, pl.ds(at, tile)] = part_ref[i]
-            j += 1
-    group = 8
+    for i, flip in enumerate(flips):
+        x_ref[:, i * tile : (i + 1) * tile] = part_ref[i]
+        tiles_ref[i * tile : (i + 1) * tile, :] = got_ref[order_ref[me ^ flip]]
+    width = x_ref.shape[1]
+    group = min(width, 8 * tile)
     total = b_ref[...]
-    for c in range(tiles // group):
-        x = x_ref[:, c * group * tile : (c + 1) * group * tile]
-        g = got_ref[c * group : (c + 1) * group].reshape(group * tile, tile)
-        total = total - dot(x, g)
+    for c in range(0, width, group):
+        total = total - dot(x_ref[:, c : c + group], tiles_ref[c : c + group, :])
     r_ref[...] = total
 
 
@@ -419,11 +415,11 @@
     small = pl.pallas_call(
         near_body,
         out_shape=held(tiles * small_rows, tile),
-        in_specs=[smem, smem, smem, vmem, vmem, hbm],
+        in_specs=[smem, smem, smem, vmem, hbm],
         out_specs=vmem,
         scratch_shapes=[pltpu.VMEM((2, tile, tile), f32), pltpu.SemaphoreType.DMA((2,))],
         name="near",
-    )(me, tile_order, block_lengths, inner_order, right_sides.T, normal_matrix)
+    )(me, tile_order, block_lengths, right_sides.T, normal_matrix)
     small_got = exchange(small, small_rows)
     tiles_out = pl.pallas_call(
         pack_body,
@@ -439,7 +435,7 @@
         out_shape=held(tiles, routed_rows, tile),
         in_specs=[smem, smem, vmem],
         out_specs=vmem,
-        scratch_shapes=[pltpu.SMEM((tiles,), jnp.int32)],
+        scratch_shapes=[pltpu.SMEM((tiles + MOSTT,), jnp.int32)],
         name="route",
     )(tile_order, block_lengths, hold(small_got))
     block_parts = exchange(routed, routed_rows)
@@ -448,7 +444,7 @@
     inverse_rows, own_sides, z = pl.pallas_call(
         lambda *refs: factor_body(*refs, per_piece=per_piece),
         out_shape=(held(tile, MOSTT * tile), held(rhs, tile), held(rhs, tile)),
-        in_specs=[smem, smem, vmem],
+        in_specs=[smem, smem, vmem, vmem],
         out_specs=(vmem, vmem, vmem),
         scratch_shapes=[
             pltpu.VMEM((MOSTT, tile, tile), f32),
@@ -457,7 +453,7 @@
         ],
         name="factor",
         compiler_params=room(1),
-    )(me, block_lengths, hold(block_parts))
+    )(me, block_lengths, inner_order, hold(block_parts))
 
     iterate, flips = spread(z)
     slab = pl.pallas_call(
@@ -469,15 +465,26 @@
         name="arrange",
     compiler_params=room(1),
     )(tile_order, hold(tiles_got))
-    residual = pl.pallas_call(
-        lambda *refs: residual_body(*refs, flips=flips),
-        out_shape=held(rhs, tile),
-        in_specs=[smem, smem, vmem, vmem] + [vmem] * len(iterate),
-        out_specs=vmem,
-        scratch_shapes=[pltpu.VMEM((rhs, tiles * tile), f32)],
-        name="residual",
-        compiler_params=room(3),
-    )(me, tile_order, hold(tiles_got), hold(own_sides), *map(hold, iterate))
+
+    def subtract(left, part, chosen):
+        return pl.pallas_call(
+            lambda *refs: residual_body(*refs, flips=chosen),
+            out_shape=held(rhs, tile),
+            in_specs=[smem, smem, vmem, vmem, vmem],
+            out_specs=vmem,
+            scratch_shapes=[
+                pltpu.VMEM((rhs, len(chosen) * tile), f32),
+                pltpu.VMEM((len(chosen) * tile, tile), f32),
+            ],
+            name="residual",
+            compiler_params=room(3),
+        )(me, tile_order, hold(tiles_got), hold(left), hold(part))
+
+    residual = own_sides
+    for part in iterate[:-1]:
+        residual = subtract(residual, part, flips[: part.shape[0]])
+        flips = flips[part.shape[0] :]
+    residual = subtract(residual, iterate[-1], flips)
     near = [
         residual if o == 0 else shift(residual, -o) for o in range(1 - MOSTT, MOSTT)
     ]

time: 108 us -> 107 us (level)
  waiting for transfers between devices: 32.6 us -> 27.2 us
  starting transfers between devices: 17.8 us -> 21.7 us
    ppermute x6, waiting for transfers between devices: 23.7 us -> 18.3 us  [swap(): return lax.ppermute(value, AXES, [(s, s ^ bit) for s in range(count)])]
    ppermute x6, starting transfers between devices: 7.5 us -> 11.4 us  [swap(): return lax.ppermute(value, AXES, [(s, s ^ bit) for s in range(count)])]
    pallas_call x1 -> x2, Pallas kernels: 1.64 us -> 2.23 us  [subtract(): pl.pallas_call(lambda *refs: residual_body(*refs, flips=chosen), out_shap...]
  transfers between devices with their start and end apart: 12 -> 12, of which waited for: 8 -> 8; matrix products, arithmetic and copies ran while one was open for 0% -> 0% of each run, Pallas kernels for 32% -> 34%
where the time goes in v4:
time: 107 us; the launch traced here: 106 us
  Pallas kernels  41.7 us (39%)
  waiting for transfers between devices  27.2 us (25%)
  starting transfers between devices  21.7 us (20%)
  blocking collectives  14.9 us (14%)
    pallas_call x1, Pallas kernels, body(): pl.pallas_call(lambda *refs: factor_body(*refs, per_piece=per_piece), out...  25 us
    ppermute x6, waiting for transfers between devices, swap(): return lax.ppermute(value, AXES, [(s, s ^ bit) for s in range(count)])  18.3 us
    all_to_all x1, blocking collectives, exchange(): moved = lax.all_to_all(value.reshape(-1, lanes), AXES, 0, 0, tiled=True)  14.9 us
    ppermute x6, starting transfers between devices, swap(): return lax.ppermute(value, AXES, [(s, s ^ bit) for s in range(count)])  11.4 us
    pallas_call x1, Pallas kernels, body(): pl.pallas_call(pack_body, out_shape=shape(tiles, tile, tile), in_specs=[s...  7.39 us
    all_to_all x2, waiting for transfers between devices, exchange(): moved = lax.all_to_all(value.reshape(-1, lanes), AXES, 0, 0, tiled=True)  6.03 us
    all_to_all x2, starting transfers between devices, exchange(): moved = lax.all_to_all(value.reshape(-1, lanes), AXES, 0, 0, tiled=True)  5.32 us
    ppermute x4, starting transfers between devices, shift(): return lax.ppermute(value, AXES, pairs)  5 us
  transfers between devices with their start and end apart: 12, of which 8 were waited for; matrix products, arithmetic and copies ran while one was open for 0% of the time, Pallas kernels for 34%

profile of v4, /device:TPU:0, one launch (start us, length us, event | category | flops | bytes accessed | tf_op | source)
XLA Modules:
  0.0 106.3 jit_solution(5127139963612199246)
XLA Ops:
  0.6 1.7 %near.1 = f32[256,128]{1,0:T(8,128)S(1)} custom-call(s32[1]{0:T(128)} %bitcast.self_ref.refs_0_, s32[32]{0:T(128)} %refs_1_.7, s32[16]{0:T(128)} %lengths_ref.3, f32[32,128]{1,0:T(8,128)} %bitcast.10, f32[128,4096]{1,0:T(8,128)} %slab_ref.3), custom_call_target="tpu_custom_call" | custom-call | tf_op jit(solution)/shard_map/near/pallas_call | solution.py:415
  2.3 14.9 %all_to_all.21.refs_2_ = f32[32,8,128]{2,1,0:T(8,128)S(1)} all-to-all(f32[32,8,128]{2,1,0:T(8,128)S(1)} %bitcast.6), channel_id=1, replica_groups=mesh['gx'=4,'gy'=8] {'gx','gy'}, dimensions={0} | all-to-all | bytes 262144 | tf_op jit(solution)/shard_map/all_to_all | solution.py:356
  17.3 1.7 %route.1 = f32[32,24,128]{2,1,0:T(8,128)} custom-call(s32[32]{0:T(128)} %refs_1_.7, s32[16]{0:T(128)} %lengths_ref.3, f32[32,8,128]{2,1,0:T(8,128)S(1)} %all_to_all.21.refs_2_), custom_call_target="tpu_custom_call" | custom-call | tf_op jit(solution)/shard_map/route/pallas_call | solution.py:433
  19.0 2.6 %all-to-all-start.2 = ((f32[32,24,128]{2,1,0:T(8,128)}), f32[32,24,128]{2,1,0:T(8,128)S(1)}, u32[]{:S(2)}, u32[]{:S(2)}) async-start(f32[32,24,128]{2,1,0:T(8,128)} %route.1), calls=%async_computation.2 | async-start | bytes 786432 | tf_op jit(solution)/shard_map/all_to_all | solution.py:356
  21.6 7.4 %pack.1 = f32[32,128,128]{2,1,0:T(8,128)} custom-call(s32[1]{0:T(128)} %bitcast.self_ref.refs_0_, s32[32]{0:T(128)} %refs_1_.7, s32[32,128]{1,0:T(8,128)} %refs_2_.1, f32[128,4096]{1,0:T(8,128)} %slab_ref.3), custom_call_target="tpu_custom_call" | custom-call | tf_op jit(solution)/shard_map/pack/pallas_call | solution.py:424
  29.0 6.0 %all-to-all-done.2.refs_3_ = f32[32,24,128]{2,1,0:T(8,128)S(1)} async-done(((f32[32,24,128]{2,1,0:T(8,128)}), f32[32,24,128]{2,1,0:T(8,128)S(1)}, u32[]{:S(2)}, u32[]{:S(2)}) %all-to-all-start.2) | async-done | bytes 393248 | tf_op jit(solution)/shard_map/all_to_all | solution.py:356
  35.0 2.7 %all-to-all-start = ((f32[32,128,128]{2,1,0:T(8,128)}), f32[32,128,128]{2,1,0:T(8,128)S(1)}, u32[]{:S(2)}, u32[]{:S(2)}) async-start(f32[32,128,128]{2,1,0:T(8,128)} %pack.1), calls=%async_computation | async-start | bytes 4194304 | tf_op jit(solution)/shard_map/all_to_all | solution.py:356
  37.8 25.0 %factor.1 = (f32[128,384]{1,0:T(8,128)S(1)}, f32[32,128]{1,0:T(8,128)S(1)}, f32[32,128]{1,0:T(8,128)S(1)}) custom-call(s32[1]{0:T(128)} %bitcast.self_ref.refs_0_, s32[16]{0:T(128)S(1)} %copy-done.2, s32[32,128]{1,0:T(8,128)S(1)} %copy-done, f32[32,24,128]{2,1,0:T(8,128)S(1)} %all-to-all-done.2.refs_3_), custom_call_target="tpu_custom_call" | custom-call | tf_op jit(solution)/shard_map/factor/pallas_call | solution.py:444
  62.8 1.7 %collective-permute-start = (f32[1,32,128]{2,1,0:T(8,128)S(1)}, f32[1,32,128]{2,1,0:T(8,128)S(1)}, u32[]{:S(2)}, u32[]{:S(2)}) collective-permute-start(f32[1,32,128]{2,1,0:T(8,128)S(1)} %bitcast.7), channel_id=1, source_target_pairs={{0,16},{1,17},{2,18},{3,19},{4,20},{5,21},{6,22},{7,23},{8,24},{9,... | collective-permute-start | bytes 49160 | tf_op jit(solution)/shard_map/ppermute | solution.py:366
  64.5 2.2 %collective-permute-done = f32[1,32,128]{2,1,0:T(8,128)S(1)} collective-permute-done((f32[1,32,128]{2,1,0:T(8,128)S(1)}, f32[1,32,128]{2,1,0:T(8,128)S(1)}, u32[]{:S(2)}, u32[]{:S(2)}) %collective-permute-start) | collective-permute-done | bytes 16416 | tf_op jit(solution)/shard_map/ppermute | solution.py:366
  66.7 1.6 %collective-permute-start.1 = (f32[2,32,128]{2,1,0:T(8,128)S(1)}, f32[2,32,128]{2,1,0:T(8,128)S(1)}, u32[]{:S(2)}, u32[]{:S(2)}) collective-permute-start(f32[2,32,128]{2,1,0:T(8,128)S(1)} %pad_maximum_fusion.1), channel_id=1, source_target_pairs={{0,1},{1,0},{2,3},{3,2},{4,5},{5,4},{6,7},{7,6},{8,9},{9,8},{10,11... | collective-permute-start | bytes 98312 | tf_op jit(solution)/shard_map/ppermute | solution.py:366
  68.4 2.3 %collective-permute-done.1 = f32[2,32,128]{2,1,0:T(8,128)S(1)} collective-permute-done((f32[2,32,128]{2,1,0:T(8,128)S(1)}, f32[2,32,128]{2,1,0:T(8,128)S(1)}, u32[]{:S(2)}, u32[]{:S(2)}) %collective-permute-start.1) | collective-permute-done | bytes 32800 | tf_op jit(solution)/shard_map/ppermute | solution.py:366
  70.7 3.6 %collective-permute-start.4 = (f32[4,32,128]{2,1,0:T(8,128)S(1)}, f32[4,32,128]{2,1,0:T(8,128)S(1)}, u32[]{:S(2)}, u32[]{:S(2)}) collective-permute-start(f32[4,32,128]{2,1,0:T(8,128)S(1)} %pad_maximum_fusion), channel_id=1, source_target_pairs={{0,6},{1,7},{2,4},{3,5},{4,2},{5,3},{6,0},{7,1},{8,14},{9,15},{10,... | collective-permute-start | bytes 196616 | tf_op jit(solution)/shard_map/ppermute | solution.py:366
  74.3 3.9 %collective-permute-start.3 = (f32[4,32,128]{2,1,0:T(8,128)S(1)}, f32[4,32,128]{2,1,0:T(8,128)S(1)}, u32[]{:S(2)}, u32[]{:S(2)}) collective-permute-start(f32[4,32,128]{2,1,0:T(8,128)S(1)} %pad_maximum_fusion), channel_id=1, source_target_pairs={{0,4},{1,5},{2,6},{3,7},{4,0},{5,1},{6,2},{7,3},{8,12},{9,13},{10,... | collective-permute-start | bytes 196616 | tf_op jit(solution)/shard_map/ppermute | solution.py:366
  78.6 4.1 %collective-permute-done.2 = f32[4,32,128]{2,1,0:T(8,128)S(1)} collective-permute-done((f32[4,32,128]{2,1,0:T(8,128)S(1)}, f32[4,32,128]{2,1,0:T(8,128)S(1)}, u32[]{:S(2)}, u32[]{:S(2)}) %collective-permute-start.2) | collective-permute-done | bytes 65568 | tf_op jit(solution)/shard_map/ppermute | solution.py:366
  82.7 9.3 %collective-permute-done.3 = f32[4,32,128]{2,1,0:T(8,128)S(1)} collective-permute-done((f32[4,32,128]{2,1,0:T(8,128)S(1)}, f32[4,32,128]{2,1,0:T(8,128)S(1)}, u32[]{:S(2)}, u32[]{:S(2)}) %collective-permute-start.3) | collective-permute-done | bytes 65568 | tf_op jit(solution)/shard_map/ppermute | solution.py:366
  92.1 1.1 %residual.2.refs_3_ = f32[32,128]{1,0:T(8,128)S(1)} custom-call(s32[1]{0:T(128)} %bitcast.self_ref.refs_0_, s32[32]{0:T(128)S(1)} %copy-done.1, f32[32,128,128]{2,1,0:T(8,128)S(1)} %all-to-all-done.got_ref.refs_2_, f32[32,128]{1,0:T(8,128)S(1)} %get-tuple-element.7.refs_3_, f32[16,32,128]{2,1,0:T(8,128)S(1)} %constant_dynamic-update-slice_fusion.refs_4_), custom_call_target="tpu_custom_call" | custom-call | tf_op jit(solution)/shard_map/residual/pallas_call | solution.py:470
  93.6 1.1 %residual.3.rest_2_ = f32[32,128]{1,0:T(8,128)S(1)} custom-call(s32[1]{0:T(128)} %bitcast.self_ref.refs_0_, s32[32]{0:T(128)S(1)} %copy-done.1, f32[32,128,128]{2,1,0:T(8,128)S(1)} %all-to-all-done.got_ref.refs_2_, f32[32,128]{1,0:T(8,128)S(1)} %residual.2.refs_3_, f32[16,32,128]{2,1,0:T(8,128)S(1)} %collective-permute-done.5.refs_4_), custom_call_target="tpu_custom_call" | custom-call | tf_op jit(solution)/shard_map/residual/pallas_call | solution.py:470
  94.8 2.1 %collective-permute-start.9 = (f32[32,128]{1,0:T(8,128)S(1)}, f32[32,128]{1,0:T(8,128)S(1)}, u32[]{:S(2)}, u32[]{:S(2)}) collective-permute-start(f32[32,128]{1,0:T(8,128)S(1)} %residual.3.rest_2_), channel_id=1, source_target_pairs={{0,30},{1,31},{2,0},{3,1},{4,2},{5,3},{6,4},{7,5},{8,6},{9,7},{10,... | collective-permute-start | bytes 49160 | tf_op jit(solution)/shard_map/ppermute | solution.py:351
  96.9 1.0 collective-permute-start.8
  97.8 1.1 %collective-permute-start.7 = (f32[32,128]{1,0:T(8,128)S(1)}, f32[32,128]{1,0:T(8,128)S(1)}, u32[]{:S(2)}, u32[]{:S(2)}) collective-permute-start(f32[32,128]{1,0:T(8,128)S(1)} %residual.3.rest_2_), channel_id=1, source_target_pairs={{0,1},{1,2},{2,3},{3,4},{4,5},{5,6},{6,7},{7,8},{8,9},{9,10},{10,1... | collective-permute-start | bytes 49160 | tf_op jit(solution)/shard_map/ppermute | solution.py:351
  99.8 2.1 %arrange.1 = f32[4096,128]{1,0:T(8,128)} custom-call(s32[32]{0:T(128)S(1)} %copy-done.1, f32[32,128,128]{2,1,0:T(8,128)S(1)} %all-to-all-done.got_ref.refs_2_), custom_call_target="tpu_custom_call" | custom-call | tf_op jit(solution)/shard_map/arrange/pallas_call | solution.py:459
  101.9 2.7 %collective-permute-done.7.rest_1_ = f32[32,128]{1,0:T(8,128)S(1)} collective-permute-done((f32[32,128]{1,0:T(8,128)S(1)}, f32[32,128]{1,0:T(8,128)S(1)}, u32[]{:S(2)}, u32[]{:S(2)}) %collective-permute-start.7) | collective-permute-done | bytes 16416 | tf_op jit(solution)/shard_map/ppermute | solution.py:351
  104.7 1.5 %finish.1 = f32[32,128]{1,0:T(8,128)} custom-call(s32[1]{0:T(128)} %bitcast.self_ref.refs_0_, s32[16]{0:T(128)S(1)} %copy-done.2, f32[128,384]{1,0:T(8,128)S(1)} %get-tuple-element.5.v_ref, f32[32,128]{1,0:T(8,128)S(1)} %get-tuple-element.6.z_ref, f32[32,128]{1,0:T(8,128)S(1)} %collective-permute-done.6.rest_0_, ...), custom_call_target="tpu_custom_call" | custom-call | tf_op jit(solution)/shard_map/finish/pallas_call | solution.py:491
  (23 shorter events, 2.1 us)
Async XLA Ops:
  19.0 16.0 %all-to-all-start.2 = ((f32[32,24,128]{2,1,0:T(8,128)}), f32[32,24,128]{2,1,0:T(8,128)S(1)}, u32[]{:S(2)}, u32[]{:S(2)}) async-start(f32[32,24,128]{2,1,0:T(8,128)} %route.1), calls=%async_computation.2 | async-start | bytes 786432 | tf_op jit(solution)/shard_map/all_to_all | solution.py:356
  29.0 8.8 %copy-start = (s32[32,128]{1,0:T(8,128)S(1)}, s32[32,128]{1,0:T(8,128)}, u32[]{:S(2)}) copy-start(s32[32,128]{1,0:T(8,128)} %refs_2_.1) | copy-start | bytes 49156
  29.0 8.8 %copy-start.2 = (s32[16]{0:T(128)S(1)}, s32[16]{0:T(128)}, u32[]{:S(2)}) copy-start(s32[16]{0:T(128)} %lengths_ref.3) | copy-start | bytes 196
  29.0 63.2 %copy-start.1 = (s32[32]{0:T(128)S(1)}, s32[32]{0:T(128)}, u32[]{:S(2)}) copy-start(s32[32]{0:T(128)} %refs_1_.7) | copy-start | bytes 388
  35.0 57.1 %all-to-all-start = ((f32[32,128,128]{2,1,0:T(8,128)}), f32[32,128,128]{2,1,0:T(8,128)S(1)}, u32[]{:S(2)}, u32[]{:S(2)}) async-start(f32[32,128,128]{2,1,0:T(8,128)} %pack.1), calls=%async_computation | async-start | bytes 4194304 | tf_op jit(solution)/shard_map/all_to_all | solution.py:356
  62.8 3.9 %collective-permute-start = (f32[1,32,128]{2,1,0:T(8,128)S(1)}, f32[1,32,128]{2,1,0:T(8,128)S(1)}, u32[]{:S(2)}, u32[]{:S(2)}) collective-permute-start(f32[1,32,128]{2,1,0:T(8,128)S(1)} %bitcast.7), channel_id=1, source_target_pairs={{0,16},{1,17},{2,18},{3,19},{4,20},{5,21},{6,22},{7,23},{8,24},{9,... | collective-permute-start | bytes 49160 | tf_op jit(solution)/shard_map/ppermute | solution.py:366
  66.7 3.9 %collective-permute-start.1 = (f32[2,32,128]{2,1,0:T(8,128)S(1)}, f32[2,32,128]{2,1,0:T(8,128)S(1)}, u32[]{:S(2)}, u32[]{:S(2)}) collective-permute-start(f32[2,32,128]{2,1,0:T(8,128)S(1)} %pad_maximum_fusion.1), channel_id=1, source_target_pairs={{0,1},{1,0},{2,3},{3,2},{4,5},{5,4},{6,7},{7,6},{8,9},{9,8},{10,11... | collective-permute-start | bytes 98312 | tf_op jit(solution)/shard_map/ppermute | solution.py:366
  70.7 21.4 %collective-permute-start.4 = (f32[4,32,128]{2,1,0:T(8,128)S(1)}, f32[4,32,128]{2,1,0:T(8,128)S(1)}, u32[]{:S(2)}, u32[]{:S(2)}) collective-permute-start(f32[4,32,128]{2,1,0:T(8,128)S(1)} %pad_maximum_fusion), channel_id=1, source_target_pairs={{0,6},{1,7},{2,4},{3,5},{4,2},{5,3},{6,0},{7,1},{8,14},{9,15},{10,... | collective-permute-start | bytes 196616 | tf_op jit(solution)/shard_map/ppermute | solution.py:366
  74.3 17.8 %collective-permute-start.3 = (f32[4,32,128]{2,1,0:T(8,128)S(1)}, f32[4,32,128]{2,1,0:T(8,128)S(1)}, u32[]{:S(2)}, u32[]{:S(2)}) collective-permute-start(f32[4,32,128]{2,1,0:T(8,128)S(1)} %pad_maximum_fusion), channel_id=1, source_target_pairs={{0,4},{1,5},{2,6},{3,7},{4,0},{5,1},{6,2},{7,3},{8,12},{9,13},{10,... | collective-permute-start | bytes 196616 | tf_op jit(solution)/shard_map/ppermute | solution.py:366
  78.1 4.6 %collective-permute-start.2 = (f32[4,32,128]{2,1,0:T(8,128)S(1)}, f32[4,32,128]{2,1,0:T(8,128)S(1)}, u32[]{:S(2)}, u32[]{:S(2)}) collective-permute-start(f32[4,32,128]{2,1,0:T(8,128)S(1)} %pad_maximum_fusion), channel_id=1, source_target_pairs={{0,2},{1,3},{2,0},{3,1},{4,6},{5,7},{6,4},{7,5},{8,10},{9,11},{10,... | collective-permute-start | bytes 196616 | tf_op jit(solution)/shard_map/ppermute | solution.py:366
  92.0 1.6 %collective-permute-start.5 = (f32[16,32,128]{2,1,0:T(8,128)S(1)}, f32[16,32,128]{2,1,0:T(8,128)S(1)}, u32[]{:S(2)}, u32[]{:S(2)}) collective-permute-start(f32[16,32,128]{2,1,0:T(8,128)S(1)} %constant_dynamic-update-slice_fusion.refs_4_), channel_id=1, source_target_pairs={{0,8},{1,9},{2,10},{3,11},{4,12},{5,13},{6,14},{7,15},{8,0},{9,1},... | collective-permute-start | bytes 786440 | tf_op jit(solution)/shard_map/ppermute | solution.py:366
  94.8 7.1 %collective-permute-start.9 = (f32[32,128]{1,0:T(8,128)S(1)}, f32[32,128]{1,0:T(8,128)S(1)}, u32[]{:S(2)}, u32[]{:S(2)}) collective-permute-start(f32[32,128]{1,0:T(8,128)S(1)} %residual.3.rest_2_), channel_id=1, source_target_pairs={{0,30},{1,31},{2,0},{3,1},{4,2},{5,3},{6,4},{7,5},{8,6},{9,7},{10,... | collective-permute-start | bytes 49160 | tf_op jit(solution)/shard_map/ppermute | solution.py:351
  96.9 5.0 %collective-permute-start.8 = (f32[32,128]{1,0:T(8,128)S(1)}, f32[32,128]{1,0:T(8,128)S(1)}, u32[]{:S(2)}, u32[]{:S(2)}) collective-permute-start(f32[32,128]{1,0:T(8,128)S(1)} %residual.3.rest_2_), channel_id=1, source_target_pairs={{0,31},{1,0},{2,1},{3,2},{4,3},{5,4},{6,5},{7,6},{8,7},{9,8},{10,9... | collective-permute-start | bytes 49160 | tf_op jit(solution)/shard_map/ppermute | solution.py:351
  97.8 6.8 %collective-permute-start.7 = (f32[32,128]{1,0:T(8,128)S(1)}, f32[32,128]{1,0:T(8,128)S(1)}, u32[]{:S(2)}, u32[]{:S(2)}) collective-permute-start(f32[32,128]{1,0:T(8,128)S(1)} %residual.3.rest_2_), channel_id=1, source_target_pairs={{0,1},{1,2},{2,3},{3,4},{4,5},{5,6},{6,7},{7,8},{8,9},{9,10},{10,1... | collective-permute-start | bytes 49160 | tf_op jit(solution)/shard_map/ppermute | solution.py:351
  98.9 5.9 %collective-permute-start.6 = (f32[32,128]{1,0:T(8,128)S(1)}, f32[32,128]{1,0:T(8,128)S(1)}, u32[]{:S(2)}, u32[]{:S(2)}) collective-permute-start(f32[32,128]{1,0:T(8,128)S(1)} %residual.3.rest_2_), channel_id=1, source_target_pairs={{0,2},{1,3},{2,4},{3,5},{4,6},{5,7},{6,8},{7,9},{8,10},{9,11},{10,... | collective-permute-start | bytes 49160 | tf_op jit(solution)/shard_map/ppermute | solution.py:351

commit v5 on v4

--- a/solution.py
+++ b/solution.py
@@ -233,7 +233,7 @@
 
 
 def apply_rows(v_ref, b):
-    return dot_t(jnp.concatenate(b, axis=1), v_ref[...])
+    return dot(jnp.concatenate(b, axis=1), v_ref[...])
 
 
 def pick(position, values):
@@ -296,7 +296,7 @@
     invert_in_place(f_ref.at[2])
     rows = block_inverse(f_ref, w01, w02, w12)
     for m in range(MOSTT):
-        v_ref[:, m * tile : (m + 1) * tile] = pick(position, [rows[p][m] for p in range(MOSTT)])
+        v_ref[m * tile : (m + 1) * tile, :] = pick(position, [rows[m][p] for p in range(MOSTT)])
     b = [bs_ref[m] for m in range(MOSTT)]
     b_ref[...] = pick(position, b)
     z_ref[...] = apply_rows(v_ref, b)
@@ -332,15 +332,14 @@
 
 
 def finish_body(self_ref, lengths_ref, v_ref, z_ref, *rest):
-    near_refs, out_ref, all_ref = rest[:-2], rest[-2], rest[-1]
+    near_refs, out_ref = rest[:-1], rest[-1]
     place = self_ref[0]
     first, length = block_of(lengths_ref, place)
     position = place - first
-    for i, near_ref in enumerate(near_refs):
-        all_ref[i] = near_ref[...]
+    around = [near_ref[...] for near_ref in near_refs]
     b = []
     for m in range(MOSTT):
-        r = all_ref[jnp.clip(MOSTT - 1 + m - position, 0, len(near_refs) - 1)]
+        r = pick(position, [around[MOSTT - 1 + m - p] for p in range(MOSTT)])
         b.append(jnp.where(m < length, r, 0.0))
     out_ref[...] = z_ref[...] + apply_rows(v_ref, b)
 
@@ -443,7 +442,7 @@
 
     inverse_rows, own_sides, z = pl.pallas_call(
         lambda *refs: factor_body(*refs, per_piece=per_piece),
-        out_shape=(held(tile, MOSTT * tile), held(rhs, tile), held(rhs, tile)),
+        out_shape=(held(MOSTT * tile, tile), held(rhs, tile), held(rhs, tile)),
         in_specs=[smem, smem, vmem, vmem],
         out_specs=(vmem, vmem, vmem),
         scratch_shapes=[
@@ -493,7 +492,6 @@
         out_shape=shape(rhs, tile),
         in_specs=[smem, smem, vmem, vmem] + [vmem] * len(near),
         out_specs=vmem,
-        scratch_shapes=[pltpu.VMEM((len(near), rhs, tile), f32)],
         name="finish",
         compiler_params=room(0.5),
     )(me, block_lengths, hold(inverse_rows), hold(z), *map(hold, near))

time: 107 us -> 107 us (level)
  transfers between devices with their start and end apart: 12 -> 12, of which waited for: 8 -> 8; matrix products, arithmetic and copies ran while one was open for 0% -> 0% of each run, Pallas kernels for 34% -> 33%
where the time goes in v5:
time: 107 us; the launch traced here: 106 us
  Pallas kernels  41.5 us (39%)
  waiting for transfers between devices  27.6 us (26%)
  starting transfers between devices  21.3 us (20%)
  blocking collectives  14.9 us (14%)
    pallas_call x1, Pallas kernels, body(): pl.pallas_call(lambda *refs: factor_body(*refs, per_piece=per_piece), out...  25 us
    ppermute x6, waiting for transfers between devices, swap(): return lax.ppermute(value, AXES, [(s, s ^ bit) for s in range(count)])  18.8 us
    all_to_all x1, blocking collectives, exchange(): moved = lax.all_to_all(value.reshape(-1, lanes), AXES, 0, 0, tiled=True)  14.9 us
    ppermute x6, starting transfers between devices, swap(): return lax.ppermute(value, AXES, [(s, s ^ bit) for s in range(count)])  11 us
    pallas_call x1, Pallas kernels, body(): pl.pallas_call(pack_body, out_shape=shape(tiles, tile, tile), in_specs=[s...  7.39 us
    all_to_all x2, waiting for transfers between devices, exchange(): moved = lax.all_to_all(value.reshape(-1, lanes), AXES, 0, 0, tiled=True)  6.03 us
    all_to_all x2, starting transfers between devices, exchange(): moved = lax.all_to_all(value.reshape(-1, lanes), AXES, 0, 0, tiled=True)  5.32 us
    ppermute x4, starting transfers between devices, shift(): return lax.ppermute(value, AXES, pairs)  5 us
  transfers between devices with their start and end apart: 12, of which 8 were waited for; matrix products, arithmetic and copies ran while one was open for 0% of the time, Pallas kernels for 33%

profile of v5, /device:TPU:0, one launch (start us, length us, event | category | flops | bytes accessed | tf_op | source)
XLA Modules:
  0.0 106.2 jit_solution(11526369467757105035)
XLA Ops:
  0.6 1.7 %near.1 = f32[256,128]{1,0:T(8,128)S(1)} custom-call(s32[1]{0:T(128)} %bitcast.self_ref.refs_0_, s32[32]{0:T(128)} %refs_1_.7, s32[16]{0:T(128)} %lengths_ref.3, f32[32,128]{1,0:T(8,128)} %bitcast.10, f32[128,4096]{1,0:T(8,128)} %slab_ref.3), custom_call_target="tpu_custom_call" | custom-call | tf_op jit(solution)/shard_map/near/pallas_call | solution.py:414
  2.3 14.9 %all_to_all.21.refs_2_ = f32[32,8,128]{2,1,0:T(8,128)S(1)} all-to-all(f32[32,8,128]{2,1,0:T(8,128)S(1)} %bitcast.6), channel_id=1, replica_groups=mesh['gx'=4,'gy'=8] {'gx','gy'}, dimensions={0} | all-to-all | bytes 262144 | tf_op jit(solution)/shard_map/all_to_all | solution.py:355
  17.3 1.7 %route.1 = f32[32,24,128]{2,1,0:T(8,128)} custom-call(s32[32]{0:T(128)} %refs_1_.7, s32[16]{0:T(128)} %lengths_ref.3, f32[32,8,128]{2,1,0:T(8,128)S(1)} %all_to_all.21.refs_2_), custom_call_target="tpu_custom_call" | custom-call | tf_op jit(solution)/shard_map/route/pallas_call | solution.py:432
  19.0 2.6 %all-to-all-start.2 = ((f32[32,24,128]{2,1,0:T(8,128)}), f32[32,24,128]{2,1,0:T(8,128)S(1)}, u32[]{:S(2)}, u32[]{:S(2)}) async-start(f32[32,24,128]{2,1,0:T(8,128)} %route.1), calls=%async_computation.2 | async-start | bytes 786432 | tf_op jit(solution)/shard_map/all_to_all | solution.py:355
  21.6 7.4 %pack.1 = f32[32,128,128]{2,1,0:T(8,128)} custom-call(s32[1]{0:T(128)} %bitcast.self_ref.refs_0_, s32[32]{0:T(128)} %refs_1_.7, s32[32,128]{1,0:T(8,128)} %refs_2_.1, f32[128,4096]{1,0:T(8,128)} %slab_ref.3), custom_call_target="tpu_custom_call" | custom-call | tf_op jit(solution)/shard_map/pack/pallas_call | solution.py:423
  29.0 6.0 %all-to-all-done.2.refs_3_ = f32[32,24,128]{2,1,0:T(8,128)S(1)} async-done(((f32[32,24,128]{2,1,0:T(8,128)}), f32[32,24,128]{2,1,0:T(8,128)S(1)}, u32[]{:S(2)}, u32[]{:S(2)}) %all-to-all-start.2) | async-done | bytes 393248 | tf_op jit(solution)/shard_map/all_to_all | solution.py:355
  35.0 2.7 %all-to-all-start = ((f32[32,128,128]{2,1,0:T(8,128)}), f32[32,128,128]{2,1,0:T(8,128)S(1)}, u32[]{:S(2)}, u32[]{:S(2)}) async-start(f32[32,128,128]{2,1,0:T(8,128)} %pack.1), calls=%async_computation | async-start | bytes 4194304 | tf_op jit(solution)/shard_map/all_to_all | solution.py:355
  37.8 25.0 %factor.1 = (f32[384,128]{1,0:T(8,128)S(1)}, f32[32,128]{1,0:T(8,128)S(1)}, f32[32,128]{1,0:T(8,128)S(1)}) custom-call(s32[1]{0:T(128)} %bitcast.self_ref.refs_0_, s32[16]{0:T(128)S(1)} %copy-done.2, s32[32,128]{1,0:T(8,128)S(1)} %copy-done, f32[32,24,128]{2,1,0:T(8,128)S(1)} %all-to-all-done.2.refs_3_), custom_call_target="tpu_custom_call" | custom-call | tf_op jit(solution)/shard_map/factor/pallas_call | solution.py:443
  62.7 1.6 %collective-permute-start = (f32[1,32,128]{2,1,0:T(8,128)S(1)}, f32[1,32,128]{2,1,0:T(8,128)S(1)}, u32[]{:S(2)}, u32[]{:S(2)}) collective-permute-start(f32[1,32,128]{2,1,0:T(8,128)S(1)} %bitcast.7), channel_id=1, source_target_pairs={{0,16},{1,17},{2,18},{3,19},{4,20},{5,21},{6,22},{7,23},{8,24},{9,... | collective-permute-start | bytes 49160 | tf_op jit(solution)/shard_map/ppermute | solution.py:365
  64.3 2.4 %collective-permute-done = f32[1,32,128]{2,1,0:T(8,128)S(1)} collective-permute-done((f32[1,32,128]{2,1,0:T(8,128)S(1)}, f32[1,32,128]{2,1,0:T(8,128)S(1)}, u32[]{:S(2)}, u32[]{:S(2)}) %collective-permute-start) | collective-permute-done | bytes 16416 | tf_op jit(solution)/shard_map/ppermute | solution.py:365
  66.7 1.4 %collective-permute-start.1 = (f32[2,32,128]{2,1,0:T(8,128)S(1)}, f32[2,32,128]{2,1,0:T(8,128)S(1)}, u32[]{:S(2)}, u32[]{:S(2)}) collective-permute-start(f32[2,32,128]{2,1,0:T(8,128)S(1)} %pad_maximum_fusion.1), channel_id=1, source_target_pairs={{0,1},{1,0},{2,3},{3,2},{4,5},{5,4},{6,7},{7,6},{8,9},{9,8},{10,11... | collective-permute-start | bytes 98312 | tf_op jit(solution)/shard_map/ppermute | solution.py:365
  68.1 2.5 %collective-permute-done.1 = f32[2,32,128]{2,1,0:T(8,128)S(1)} collective-permute-done((f32[2,32,128]{2,1,0:T(8,128)S(1)}, f32[2,32,128]{2,1,0:T(8,128)S(1)}, u32[]{:S(2)}, u32[]{:S(2)}) %collective-permute-start.1) | collective-permute-done | bytes 32800 | tf_op jit(solution)/shard_map/ppermute | solution.py:365
  70.6 3.5 %collective-permute-start.4 = (f32[4,32,128]{2,1,0:T(8,128)S(1)}, f32[4,32,128]{2,1,0:T(8,128)S(1)}, u32[]{:S(2)}, u32[]{:S(2)}) collective-permute-start(f32[4,32,128]{2,1,0:T(8,128)S(1)} %pad_maximum_fusion), channel_id=1, source_target_pairs={{0,6},{1,7},{2,4},{3,5},{4,2},{5,3},{6,0},{7,1},{8,14},{9,15},{10,... | collective-permute-start | bytes 196616 | tf_op jit(solution)/shard_map/ppermute | solution.py:365
  74.1 3.9 %collective-permute-start.3 = (f32[4,32,128]{2,1,0:T(8,128)S(1)}, f32[4,32,128]{2,1,0:T(8,128)S(1)}, u32[]{:S(2)}, u32[]{:S(2)}) collective-permute-start(f32[4,32,128]{2,1,0:T(8,128)S(1)} %pad_maximum_fusion), channel_id=1, source_target_pairs={{0,4},{1,5},{2,6},{3,7},{4,0},{5,1},{6,2},{7,3},{8,12},{9,13},{10,... | collective-permute-start | bytes 196616 | tf_op jit(solution)/shard_map/ppermute | solution.py:365
  78.5 4.1 %collective-permute-done.2 = f32[4,32,128]{2,1,0:T(8,128)S(1)} collective-permute-done((f32[4,32,128]{2,1,0:T(8,128)S(1)}, f32[4,32,128]{2,1,0:T(8,128)S(1)}, u32[]{:S(2)}, u32[]{:S(2)}) %collective-permute-start.2) | collective-permute-done | bytes 65568 | tf_op jit(solution)/shard_map/ppermute | solution.py:365
  82.6 9.4 %collective-permute-done.3 = f32[4,32,128]{2,1,0:T(8,128)S(1)} collective-permute-done((f32[4,32,128]{2,1,0:T(8,128)S(1)}, f32[4,32,128]{2,1,0:T(8,128)S(1)}, u32[]{:S(2)}, u32[]{:S(2)}) %collective-permute-start.3) | collective-permute-done | bytes 65568 | tf_op jit(solution)/shard_map/ppermute | solution.py:365
  92.1 1.1 %residual.2.refs_3_ = f32[32,128]{1,0:T(8,128)S(1)} custom-call(s32[1]{0:T(128)} %bitcast.self_ref.refs_0_, s32[32]{0:T(128)S(1)} %copy-done.1, f32[32,128,128]{2,1,0:T(8,128)S(1)} %all-to-all-done.got_ref.refs_2_, f32[32,128]{1,0:T(8,128)S(1)} %get-tuple-element.7.refs_3_, f32[16,32,128]{2,1,0:T(8,128)S(1)} %constant_dynamic-update-slice_fusion.refs_4_), custom_call_target="tpu_custom_call" | custom-call | tf_op jit(solution)/shard_map/residual/pallas_call | solution.py:469
  93.6 1.1 %residual.3.rest_2_ = f32[32,128]{1,0:T(8,128)S(1)} custom-call(s32[1]{0:T(128)} %bitcast.self_ref.refs_0_, s32[32]{0:T(128)S(1)} %copy-done.1, f32[32,128,128]{2,1,0:T(8,128)S(1)} %all-to-all-done.got_ref.refs_2_, f32[32,128]{1,0:T(8,128)S(1)} %residual.2.refs_3_, f32[16,32,128]{2,1,0:T(8,128)S(1)} %collective-permute-done.5.refs_4_), custom_call_target="tpu_custom_call" | custom-call | tf_op jit(solution)/shard_map/residual/pallas_call | solution.py:469
  94.8 2.1 %collective-permute-start.9 = (f32[32,128]{1,0:T(8,128)S(1)}, f32[32,128]{1,0:T(8,128)S(1)}, u32[]{:S(2)}, u32[]{:S(2)}) collective-permute-start(f32[32,128]{1,0:T(8,128)S(1)} %residual.3.rest_2_), channel_id=1, source_target_pairs={{0,30},{1,31},{2,0},{3,1},{4,2},{5,3},{6,4},{7,5},{8,6},{9,7},{10,... | collective-permute-start | bytes 49160 | tf_op jit(solution)/shard_map/ppermute | solution.py:350
  96.9 1.0 collective-permute-start.8
  97.8 1.1 %collective-permute-start.7 = (f32[32,128]{1,0:T(8,128)S(1)}, f32[32,128]{1,0:T(8,128)S(1)}, u32[]{:S(2)}, u32[]{:S(2)}) collective-permute-start(f32[32,128]{1,0:T(8,128)S(1)} %residual.3.rest_2_), channel_id=1, source_target_pairs={{0,1},{1,2},{2,3},{3,4},{4,5},{5,6},{6,7},{7,8},{8,9},{9,10},{10,1... | collective-permute-start | bytes 49160 | tf_op jit(solution)/shard_map/ppermute | solution.py:350
  99.8 2.1 %arrange.1 = f32[4096,128]{1,0:T(8,128)} custom-call(s32[32]{0:T(128)S(1)} %copy-done.1, f32[32,128,128]{2,1,0:T(8,128)S(1)} %all-to-all-done.got_ref.refs_2_), custom_call_target="tpu_custom_call" | custom-call | tf_op jit(solution)/shard_map/arrange/pallas_call | solution.py:458
  101.9 2.7 %collective-permute-done.7.rest_1_ = f32[32,128]{1,0:T(8,128)S(1)} collective-permute-done((f32[32,128]{1,0:T(8,128)S(1)}, f32[32,128]{1,0:T(8,128)S(1)}, u32[]{:S(2)}, u32[]{:S(2)}) %collective-permute-start.7) | collective-permute-done | bytes 16416 | tf_op jit(solution)/shard_map/ppermute | solution.py:350
  104.7 1.4 %finish.1 = f32[32,128]{1,0:T(8,128)} custom-call(s32[1]{0:T(128)} %bitcast.self_ref.refs_0_, s32[16]{0:T(128)S(1)} %copy-done.2, f32[384,128]{1,0:T(8,128)S(1)} %get-tuple-element.5.v_ref, f32[32,128]{1,0:T(8,128)S(1)} %get-tuple-element.6.z_ref, f32[32,128]{1,0:T(8,128)S(1)} %collective-permute-done.6.rest_0_, ...), custom_call_target="tpu_custom_call" | custom-call | tf_op jit(solution)/shard_map/finish/pallas_call | solution.py:490
  (23 shorter events, 2.1 us)
Async XLA Ops:
  19.0 16.0 %all-to-all-start.2 = ((f32[32,24,128]{2,1,0:T(8,128)}), f32[32,24,128]{2,1,0:T(8,128)S(1)}, u32[]{:S(2)}, u32[]{:S(2)}) async-start(f32[32,24,128]{2,1,0:T(8,128)} %route.1), calls=%async_computation.2 | async-start | bytes 786432 | tf_op jit(solution)/shard_map/all_to_all | solution.py:355
  29.0 8.8 %copy-start = (s32[32,128]{1,0:T(8,128)S(1)}, s32[32,128]{1,0:T(8,128)}, u32[]{:S(2)}) copy-start(s32[32,128]{1,0:T(8,128)} %refs_2_.1) | copy-start | bytes 49156
  29.0 8.8 %copy-start.2 = (s32[16]{0:T(128)S(1)}, s32[16]{0:T(128)}, u32[]{:S(2)}) copy-start(s32[16]{0:T(128)} %lengths_ref.3) | copy-start | bytes 196
  29.0 63.2 %copy-start.1 = (s32[32]{0:T(128)S(1)}, s32[32]{0:T(128)}, u32[]{:S(2)}) copy-start(s32[32]{0:T(128)} %refs_1_.7) | copy-start | bytes 388
  35.0 57.1 %all-to-all-start = ((f32[32,128,128]{2,1,0:T(8,128)}), f32[32,128,128]{2,1,0:T(8,128)S(1)}, u32[]{:S(2)}, u32[]{:S(2)}) async-start(f32[32,128,128]{2,1,0:T(8,128)} %pack.1), calls=%async_computation | async-start | bytes 4194304 | tf_op jit(solution)/shard_map/all_to_all | solution.py:355
  62.7 4.0 %collective-permute-start = (f32[1,32,128]{2,1,0:T(8,128)S(1)}, f32[1,32,128]{2,1,0:T(8,128)S(1)}, u32[]{:S(2)}, u32[]{:S(2)}) collective-permute-start(f32[1,32,128]{2,1,0:T(8,128)S(1)} %bitcast.7), channel_id=1, source_target_pairs={{0,16},{1,17},{2,18},{3,19},{4,20},{5,21},{6,22},{7,23},{8,24},{9,... | collective-permute-start | bytes 49160 | tf_op jit(solution)/shard_map/ppermute | solution.py:365
  66.7 3.9 %collective-permute-start.1 = (f32[2,32,128]{2,1,0:T(8,128)S(1)}, f32[2,32,128]{2,1,0:T(8,128)S(1)}, u32[]{:S(2)}, u32[]{:S(2)}) collective-permute-start(f32[2,32,128]{2,1,0:T(8,128)S(1)} %pad_maximum_fusion.1), channel_id=1, source_target_pairs={{0,1},{1,0},{2,3},{3,2},{4,5},{5,4},{6,7},{7,6},{8,9},{9,8},{10,11... | collective-permute-start | bytes 98312 | tf_op jit(solution)/shard_map/ppermute | solution.py:365
  70.6 21.4 %collective-permute-start.4 = (f32[4,32,128]{2,1,0:T(8,128)S(1)}, f32[4,32,128]{2,1,0:T(8,128)S(1)}, u32[]{:S(2)}, u32[]{:S(2)}) collective-permute-start(f32[4,32,128]{2,1,0:T(8,128)S(1)} %pad_maximum_fusion), channel_id=1, source_target_pairs={{0,6},{1,7},{2,4},{3,5},{4,2},{5,3},{6,0},{7,1},{8,14},{9,15},{10,... | collective-permute-start | bytes 196616 | tf_op jit(solution)/shard_map/ppermute | solution.py:365
  74.1 17.9 %collective-permute-start.3 = (f32[4,32,128]{2,1,0:T(8,128)S(1)}, f32[4,32,128]{2,1,0:T(8,128)S(1)}, u32[]{:S(2)}, u32[]{:S(2)}) collective-permute-start(f32[4,32,128]{2,1,0:T(8,128)S(1)} %pad_maximum_fusion), channel_id=1, source_target_pairs={{0,4},{1,5},{2,6},{3,7},{4,0},{5,1},{6,2},{7,3},{8,12},{9,13},{10,... | collective-permute-start | bytes 196616 | tf_op jit(solution)/shard_map/ppermute | solution.py:365
  78.0 4.6 %collective-permute-start.2 = (f32[4,32,128]{2,1,0:T(8,128)S(1)}, f32[4,32,128]{2,1,0:T(8,128)S(1)}, u32[]{:S(2)}, u32[]{:S(2)}) collective-permute-start(f32[4,32,128]{2,1,0:T(8,128)S(1)} %pad_maximum_fusion), channel_id=1, source_target_pairs={{0,2},{1,3},{2,0},{3,1},{4,6},{5,7},{6,4},{7,5},{8,10},{9,11},{10,... | collective-permute-start | bytes 196616 | tf_op jit(solution)/shard_map/ppermute | solution.py:365
  92.0 1.6 %collective-permute-start.5 = (f32[16,32,128]{2,1,0:T(8,128)S(1)}, f32[16,32,128]{2,1,0:T(8,128)S(1)}, u32[]{:S(2)}, u32[]{:S(2)}) collective-permute-start(f32[16,32,128]{2,1,0:T(8,128)S(1)} %constant_dynamic-update-slice_fusion.refs_4_), channel_id=1, source_target_pairs={{0,8},{1,9},{2,10},{3,11},{4,12},{5,13},{6,14},{7,15},{8,0},{9,1},... | collective-permute-start | bytes 786440 | tf_op jit(solution)/shard_map/ppermute | solution.py:365
  94.8 7.1 %collective-permute-start.9 = (f32[32,128]{1,0:T(8,128)S(1)}, f32[32,128]{1,0:T(8,128)S(1)}, u32[]{:S(2)}, u32[]{:S(2)}) collective-permute-start(f32[32,128]{1,0:T(8,128)S(1)} %residual.3.rest_2_), channel_id=1, source_target_pairs={{0,30},{1,31},{2,0},{3,1},{4,2},{5,3},{6,4},{7,5},{8,6},{9,7},{10,... | collective-permute-start | bytes 49160 | tf_op jit(solution)/shard_map/ppermute | solution.py:350
  96.9 5.0 %collective-permute-start.8 = (f32[32,128]{1,0:T(8,128)S(1)}, f32[32,128]{1,0:T(8,128)S(1)}, u32[]{:S(2)}, u32[]{:S(2)}) collective-permute-start(f32[32,128]{1,0:T(8,128)S(1)} %residual.3.rest_2_), channel_id=1, source_target_pairs={{0,31},{1,0},{2,1},{3,2},{4,3},{5,4},{6,5},{7,6},{8,7},{9,8},{10,9... | collective-permute-start | bytes 49160 | tf_op jit(solution)/shard_map/ppermute | solution.py:350
  97.8 6.8 %collective-permute-start.7 = (f32[32,128]{1,0:T(8,128)S(1)}, f32[32,128]{1,0:T(8,128)S(1)}, u32[]{:S(2)}, u32[]{:S(2)}) collective-permute-start(f32[32,128]{1,0:T(8,128)S(1)} %residual.3.rest_2_), channel_id=1, source_target_pairs={{0,1},{1,2},{2,3},{3,4},{4,5},{5,6},{6,7},{7,8},{8,9},{9,10},{10,1... | collective-permute-start | bytes 49160 | tf_op jit(solution)/shard_map/ppermute | solution.py:350
  98.9 5.9 %collective-permute-start.6 = (f32[32,128]{1,0:T(8,128)S(1)}, f32[32,128]{1,0:T(8,128)S(1)}, u32[]{:S(2)}, u32[]{:S(2)}) collective-permute-start(f32[32,128]{1,0:T(8,128)S(1)} %residual.3.rest_2_), channel_id=1, source_target_pairs={{0,2},{1,3},{2,4},{3,5},{4,6},{5,7},{6,8},{7,9},{8,10},{9,11},{10,... | collective-permute-start | bytes 49160 | tf_op jit(solution)/shard_map/ppermute | solution.py:350
